TPU v7x, 128 devices: a whole 4x4x4 slice. The times are simulated.
128 devices in a mesh: dp: 1, vp: 16 (over z, y), tp: 8 (over x, core).
Axes of the slice: x: 4, y: 4, z: 4, core: 2. Of those that a mesh axis runs over, the one named last changes fastest.
Arguments:
- hidden: bfloat16 [512, 2048], P('dp', 'tp')
- lnf_gain: float32 [2048], P('tp')
- lnf_bias: float32 [2048], P('tp')
- emb_table: bfloat16 [250880, 2048], P('vp', 'tp')
- next_tok: int32 [512], P('dp')
- eln_gain: float32 [2048], P('tp')
- eln_bias: float32 [2048], P('tp')
Outputs:
- output 1: float32 [512, 250880], P('dp', ('vp', 'tp'))
- output 2: float32 [512], P('dp')
- output 3: bfloat16 [512, 2048], P('dp', 'tp')
All inputs are finite; a program needn't handle non-finite values.
Results may differ from a plain program's by a relative error of at most 0.001.
Values sent between devices are 32-bit elements.
A program may use at most 1 GiB of HBM per device.

v0:
```python
import jax
import jax.numpy as jnp
from jax import lax
from jax.sharding import PartitionSpec as P

NORM_EPS = 1e-5


def norm_shard(rows_in, norm_gain, norm_bias, full_width):
    rows_f32 = rows_in.astype(jnp.float32)
    row_sums = jnp.stack([jnp.sum(rows_f32, axis=1), jnp.sum(rows_f32 * rows_f32, axis=1)])
    row_sums = lax.psum(row_sums, "tp")
    row_mean = row_sums[0] / full_width
    row_var = row_sums[1] / full_width - row_mean * row_mean
    scaled = (rows_f32 - row_mean[:, None]) * lax.rsqrt(row_var + NORM_EPS)[:, None]
    return (scaled * norm_gain + norm_bias).astype(jnp.bfloat16)


def global_lse(logits):
    row_top = lax.pmax(jnp.max(logits, axis=1), ("vp", "tp"))
    exp_total = lax.psum(jnp.sum(jnp.exp(logits - row_top[:, None]), axis=1), ("vp", "tp"))
    return row_top + jnp.log(exp_total)


def solution(mesh):
    tp_size = mesh.shape["tp"]

    def per_device(hidden, lnf_gain, lnf_bias, emb_table, next_tok, eln_gain, eln_bias):
        full_width = hidden.shape[1] * tp_size
        normed = norm_shard(hidden, lnf_gain, lnf_bias, full_width)
        shard_logits = lax.dot_general(normed, emb_table, (((1,), (1,)), ((), ())), preferred_element_type=jnp.float32)
        logits = lax.psum_scatter(shard_logits, "tp", scatter_dimension=1, tiled=True)
        log_sum = global_lse(logits)
        logprobs = logits - log_sum[:, None]
        block_rows = emb_table.shape[0]
        local_idx = next_tok - lax.axis_index("vp") * block_rows
        is_owned = (local_idx >= 0) & (local_idx < block_rows)
        picked = jnp.take(emb_table, jnp.clip(local_idx, 0, block_rows - 1), axis=0).astype(jnp.float32)
        picked = jnp.where(is_owned[:, None], picked, jnp.zeros_like(picked))
        tok_rows = lax.psum(picked, "vp")
        next_in = norm_shard(tok_rows, eln_gain, eln_bias, full_width)
        return logprobs, log_sum, next_in

    return jax.shard_map(
        per_device,
        mesh=mesh,
        in_specs=(P("dp", "tp"), P("tp"), P("tp"), P("vp", "tp"), P("dp"), P("tp"), P("tp")),
        out_specs=(P("dp", ("vp", "tp")), P("dp"), P("dp", "tp")),
        check_vma=False,
    )
```

profile of v0, /device:TPU:1, one launch (start us, length us, event | category | flops | bytes accessed | tf_op | source)
XLA Modules:
  0.0 440.6 jit_solution(5713115405343892549)
XLA Ops:
  7.2 0.0 copy-start
  7.2 0.0 copy-start.2
  7.2 0.0 copy-start.3
  7.2 0.0 all-reduce.3.cloned.1.call-start
  7.2 0.7 compare_and_fusion
  8.0 5.9 %gather_fusion = bf16[512,256]{1,0:T(8,128)(2,1)S(1)} fusion(bf16[15680,256]{1,0:T(8,128)(2,1)} %param.10, s32[1024]{0:T(1024)S(1)} %pad_clamp_fusion), kind=kCustom, calls=%fused_computation | custom fusion | bytes 526336 | tf_op jit(solution)/shard_map/jit(_take)/gather | solution.py:38
  13.9 1.0 convert_select_fusion
  14.9 0.0 all-reduce.3.cloned.1.call-update
  14.9 0.0 reduce-scatter.2.cloned.1.call-start
  14.9 1.2 convert_reduce_fusion
  16.1 85.9 %all-reduce.3.cloned.1.call-done = f32[512,256]{1,0:T(8,128)} async-done(((f32[512,256]{1,0:T(8,128)}), f32[512,256]{1,0:T(8,128)}) %all-reduce.3.cloned.1.call-update) | async-done | bytes 524304 | tf_op jit(solution)/shard_map/psum | solution.py:40
  102.0 1.3 fusion.11
  103.3 14.4 %all-reduce = (f32[2,512]{1,0:T(2,128)S(1)}, f32[2,512]{1,0:T(2,128)S(1)}) all-reduce(f32[2,512]{1,0:T(2,128)S(1)} %pad_maximum_fusion, f32[2,512]{1,0:T(2,128)S(1)} %pad_maximum_fusion.1), channel_id=1, replica_groups=mesh['dp'=1,'vp'=16,'tp'=8] {'tp'}, use_global_device_ids=true, to_apply=%region_2.0 | all-reduce | flops 2048 | bytes 16384 | tf_op jit(solution)/shard_map/psum | solution.py:12
  117.7 0.0 copy-done
  117.7 0.0 copy-done.2
  117.7 0.0 copy-done.3
  117.7 16.3 %fusion.5 = f32[512,15680]{0,1:T(8,128)} fusion(bf16[15680,256]{1,0:T(8,128)(2,1)} %param.10, bf16[512,256]{1,0:T(8,128)(2,1)S(1)} %copy-done, f32[256]{0:T(256)S(1)} %copy-done.2, f32[256]{0:T(256)S(1)} %copy-done.3, f32[512]{0:T(512)S(1)} %add_rsqrt_fusion.1, f32[512]{0:T(512)S(1)} %bitcast.10), kind=kOutput, calls=%fused_computation.14 | convolution fusion | flops 4111204352 | bytes 40409088 | tf_op jit(solution)/shard_map/dot_general | solution.py:31
  134.0 0.0 copy-start.1
  134.0 0.0 copy-start.5
  134.0 0.0 copy-start.6
  134.0 0.0 reduce-scatter.2.cloned.1.call-update
  134.0 1.0 copy-done.1
  135.0 0.0 copy-done.5
  135.0 0.0 copy-done.6
  135.0 0.9 add_convert_fusion
  136.0 159.2 %reduce-scatter.2.cloned.1.call-done = f32[512,1960]{0,1:T(8,128)} async-done(((f32[512,15680]{0,1:T(8,128)}), f32[512,1960]{0,1:T(8,128)}) %reduce-scatter.2.cloned.1.call-update) | async-done | bytes 4014096 | tf_op jit(solution)/shard_map/reduce_scatter | solution.py:32
  295.1 2.5 reduce_max.9
  297.6 65.7 %pmax.7 = f32[512]{0:T(512)S(1)} all-reduce(f32[512]{0:T(512)S(1)} %reduce_max.9), channel_id=1, replica_groups=mesh['dp'=1,'vp'=16,'tp'=8] {'vp','tp'}, use_global_device_ids=true, to_apply=%region_5.0 | all-reduce | flops 512 | bytes 4096 | tf_op jit(solution)/shard_map/pmax | solution.py:20
  363.2 2.7 exponential_reduce_fusion
  366.0 63.1 %psum.29 = f32[512]{0:T(512)S(1)} all-reduce(f32[512]{0:T(512)S(1)} %exponential_reduce_fusion), channel_id=1, replica_groups=mesh['dp'=1,'vp'=16,'tp'=8] {'vp','tp'}, use_global_device_ids=true, to_apply=%region_7.0 | all-reduce | flops 512 | bytes 4096 | tf_op jit(solution)/shard_map/psum | solution.py:21
  429.1 4.6 %broadcast_subtract_fusion = f32[512,1960]{0,1:T(8,128)} fusion(f32[512,1960]{0,1:T(8,128)} %reduce-scatter.2.cloned.1.call-done, f32[512]{0:T(512)S(1)} %log_add_fusion), kind=kLoop, calls=%fused_computation.2 | loop fusion | flops 1003520 | bytes 8030208 | tf_op jit(solution)/shard_map/sub | solution.py:34
  433.7 0.0 copy-done.4
  (8 shorter events, 0.1 us)
Async XLA Ops:
  7.2 110.6 %copy-start = (bf16[512,256]{1,0:T(8,128)(2,1)S(1)}, bf16[512,256]{1,0:T(8,128)(2,1)}, u32[]{:S(2)}) copy-start(bf16[512,256]{1,0:T(8,128)(2,1)} %param.7) | copy-start | bytes 786436
  7.2 110.6 %copy-start.2 = (f32[256]{0:T(256)S(1)}, f32[256]{0:T(256)}, u32[]{:S(2)}) copy-start(f32[256]{0:T(256)} %param.9) | copy-start | bytes 3076
  7.2 110.6 %copy-start.3 = (f32[256]{0:T(256)S(1)}, f32[256]{0:T(256)}, u32[]{:S(2)}) copy-start(f32[256]{0:T(256)} %param.8) | copy-start | bytes 3076
  7.2 94.8 %all-reduce.3.cloned.1.call-start = ((), (), s32[]{:S(2)}) async-start(), calls=%async_computation.2 | async-start | bytes 1048576 | tf_op jit(solution)/shard_map/psum | solution.py:40
  14.9 280.2 %reduce-scatter.2.cloned.1.call-start = ((), (), s32[]{:S(2)}) async-start(), calls=%async_computation.1 | async-start | bytes 36126720 | tf_op jit(solution)/shard_map/reduce_scatter | solution.py:32
  134.0 1.0 copy-start.1
  134.0 1.0 copy-start.5
  134.0 1.0 copy-start.6
  429.1 4.6 %copy-start.4 = (f32[512]{0:T(512)}, f32[512]{0:T(512)S(1)}, u32[]{:S(2)}) copy-start(f32[512]{0:T(512)S(1)} %log_add_fusion) | copy-start | bytes 6148
Sparse Core Ops, SparseCore 0:
  15.0 86.9 all-reduce.2
  134.2 160.9 reduce-scatter.1
where the time goes:
time: 441 us
  waiting for transfers between devices  245 us (56%)
  blocking collectives  143 us (32%)
  matrix products  16.3 us (4%)
  other arithmetic  14.9 us (3%)
  between operations  14.2 us (3%)
  local copies, waits for them, and re-layouts  6.9 us (2%)
    reduce_scatter x1, waiting for transfers between devices, per_device(): lax.psum_scatter(shard_logits, 'tp', scatter_dimension=1, tiled=True)  159 us
    psum x1, waiting for transfers between devices, per_device(): tok_rows = lax.psum(picked, 'vp')  85.9 us
    pmax x1, blocking collectives, global_lse(): row_top = lax.pmax(jnp.max(logits, axis=1), ('vp', 'tp'))  65.7 us
    psum x1, blocking collectives, global_lse(): lax.psum(jnp.sum(jnp.exp(logits - row_top[:, None]), axis=1), ('vp', 'tp'))  63.1 us
    dot_general x1, matrix products, per_device(): lax.dot_general(normed, emb_table, (((1,), (1,)), ((), ())), preferred_el...  16.3 us
    psum x1, blocking collectives, norm_shard(): row_sums = lax.psum(row_sums, 'tp')  14.4 us
  transfers between devices with their start and end apart: 2, of which 2 were waited for; matrix products, arithmetic and copies ran while one was open for 0% of the time, Pallas kernels for 0%

commit v1 on v0

v1 whole, which is shorter than its diff:
```python
import functools

import jax
import jax.numpy as jnp
from jax import lax
from jax.experimental import pallas as pl
from jax.experimental.pallas import tpu as pltpu
from jax.sharding import PartitionSpec as P

NORM_EPS = 1e-5
MESH = pl.DeviceIdType.MESH
CHUNK = 128
F32 = jnp.float32
BF16 = jnp.bfloat16

OPP, LEFT, RIGHT, OWN = 0, 1, 2, 3
STEP_OF_SLOT = (2, 3, 1, 0)


def head_kernel(n_vp, n_tp, n_block, full_width,
                hid_ref, g_ref, b_ref, emb_ref, tok_ref, eg_ref, eb_ref,
                logits_ref, lse_ref, next_ref,
                e_own, e_oth, e_out, e_in, send_f, recv_f, send_n, recv_l, recv_r,
                hx, xn, m_acc, s_acc, pick, st_ln, st_lse, st_all, rs_buf, row_st, ag_buf,
                own_sem, oth_sem, ex_send, ex_recv, hx_send, hx_recv,
                f_send, f_recv, n_send, r_send, l_recv, r_recv,
                t_send, t_recv, v_send, v_recv):
    vp = lax.axis_index("vp")
    tp = lax.axis_index("tp")
    core = lax.rem(tp, 2)
    chip = tp // 2
    n_chip = n_tp // 2
    rows = hid_ref.shape[0]
    width = hid_ref.shape[1]
    slab = rows // n_vp
    left = {"tp": lax.rem(chip + n_chip - 1, n_chip) * 2 + core}
    right = {"tp": lax.rem(chip + 1, n_chip) * 2 + core}
    partner = {"tp": chip * 2 + 1 - core}
    half = (n_block // 2) // CHUNK
    n_round = half + 1
    small = n_block - 2 * half * CHUNK
    small2 = (small // 16) * 8
    small1 = small - small2
    tail0 = 2 * half * CHUNK

    def piece(h, i):
        if isinstance(i, int) and i == 0:
            return (tail0 + small2, small1) if h == 0 else (tail0, small2)
        off = h * half * CHUNK + (i - 1) * CHUNK
        return (off if isinstance(i, int) else pl.multiple_of(off, CHUNK)), CHUNK

    def load(slot, other):
        blk = lax.rem(chip + STEP_OF_SLOT[slot], n_chip) * 2 + (1 - core if other else core)
        src = emb_ref.at[pl.ds(pl.multiple_of(blk * n_block, 8), n_block), :]
        dst = (e_oth if other else e_own).at[slot]
        return pltpu.make_async_copy(src, dst, (oth_sem if other else own_sem).at[slot])

    for slot in range(4):
        load(slot, True).start()
        load(slot, False).start()

    barrier = pltpu.get_barrier_semaphore()
    for j in range(1, n_tp):
        pl.semaphore_signal(barrier, inc=1, device_id={"tp": lax.rem(tp + j, n_tp)}, device_id_type=MESH)
    for j in range(1, n_vp):
        pl.semaphore_signal(barrier, inc=1, device_id={"vp": lax.rem(vp + j, n_vp)}, device_id_type=MESH)

    h_t = hid_ref[...].astype(F32).T
    hx[0, :, 0:rows] = h_t
    hx[0, :, rows:rows + 128] = jnp.broadcast_to(g_ref[...], (128, width)).T
    hx[0, :, rows + 128:rows + 256] = jnp.broadcast_to(b_ref[...], (128, width)).T
    sub8 = lax.broadcasted_iota(jnp.int32, (8, rows), 0)
    st_ln[tp] = jnp.where(sub8 == 0, jnp.sum(h_t, axis=0, keepdims=True), jnp.sum(h_t * h_t, axis=0, keepdims=True))

    pl.semaphore_wait(barrier, n_tp + n_vp - 2)

    def tp_copy(buf, stage, j):
        peer = lax.rem(tp + j, n_tp)
        return pltpu.make_async_remote_copy(
            src_ref=buf.at[tp], dst_ref=buf.at[tp], send_sem=t_send.at[stage, j], recv_sem=t_recv.at[stage, j],
            device_id={"tp": peer}, device_id_type=MESH)

    def tp_start(buf, stage):
        for j in range(1, n_tp):
            tp_copy(buf, stage, j).start()

    def tp_wait(buf, stage):
        for j in range(1, n_tp):
            src = lax.rem(tp + n_tp - j, n_tp)
            pltpu.make_async_remote_copy(
                src_ref=buf.at[src], dst_ref=buf.at[src], send_sem=t_send.at[stage, j], recv_sem=t_recv.at[stage, j],
                device_id={"tp": src}, device_id_type=MESH).wait_recv()

    def tp_drain(buf, stage):
        for j in range(1, n_tp):
            tp_copy(buf, stage, j).wait_send()

    tp_start(st_ln, 0)

    hx_copy = pltpu.make_async_remote_copy(
        src_ref=hx.at[0], dst_ref=hx.at[1], send_sem=hx_send.at[0], recv_sem=hx_recv.at[0],
        device_id=partner, device_id_type=MESH)
    hx_copy.start()

    parts = ((tail0, small), (0, tail0))

    def ex_copy(slot, q):
        off, n = parts[q]
        return pltpu.make_async_remote_copy(
            src_ref=e_out.at[slot, pl.ds(off, n), :], dst_ref=e_in.at[slot, pl.ds(off, n), :],
            send_sem=ex_send.at[slot, q], recv_sem=ex_recv.at[slot, q], device_id=partner, device_id_type=MESH)

    for slot in range(4):
        load(slot, True).wait()
        for q in range(2):
            off, n = parts[q]
            e_out[slot, off:off + n, :] = e_oth[slot, off:off + n, :].astype(F32)
            ex_copy(slot, q).start()

    tp_wait(st_ln, 0)
    total = st_ln[0]
    for j in range(1, n_tp):
        total = total + st_ln[j]
    mean = total[0:1] / full_width
    rstd = lax.rsqrt(total[1:2] / full_width - mean * mean + NORM_EPS)

    def norm(which):
        gain = hx[which, :, rows:rows + 128]
        bias = hx[which, :, rows + 128:rows + 256]
        for c in range(rows // 128):
            cols = slice(c * 128, c * 128 + 128)
            xn[which, :, cols] = ((hx[which, :, cols] - mean[:, cols]) * rstd[:, cols] * gain + bias).astype(BF16)

    norm(0)
    hx_copy.wait_recv()
    norm(1)

    def part_sum(slot, off, n):
        mine = e_own[slot, pl.ds(off, n), :]
        theirs = e_in[slot, pl.ds(off, n), :].astype(BF16)
        return (jnp.dot(mine, xn[0], preferred_element_type=F32)
                + jnp.dot(theirs, xn[1], preferred_element_type=F32))

    def f_copy(h, i):
        off, n = piece(h, i)
        return pltpu.make_async_remote_copy(
            src_ref=send_f.at[pl.ds(off, n), :], dst_ref=recv_f.at[pl.ds(off, n), :],
            send_sem=f_send.at[h, i], recv_sem=f_recv.at[h, i],
            device_id=left if h == 0 else right, device_id_type=MESH)

    def r_copy(h, i):
        off, n = piece(h, i)
        dst = (recv_r if h == 0 else recv_l).at[pl.ds(off, n), :]
        return pltpu.make_async_remote_copy(
            src_ref=recv_f.at[pl.ds(off, n), :], dst_ref=dst,
            send_sem=r_send.at[h, i], recv_sem=(r_recv if h == 0 else l_recv).at[h, i],
            device_id=left if h == 0 else right, device_id_type=MESH)

    def n_copy(h, i):
        off, n = piece(h, i)
        dst = (recv_l if h == 0 else recv_r).at[pl.ds(off, n), :]
        return pltpu.make_async_remote_copy(
            src_ref=send_n.at[pl.ds(off, n), :], dst_ref=dst,
            send_sem=n_send.at[h, i], recv_sem=(l_recv if h == 0 else r_recv).at[h, i],
            device_id=right if h == 0 else left, device_id_type=MESH)

    def far(i):
        for h in range(2):
            off, n = piece(h, i)
            send_f[pl.ds(off, n), :] = part_sum(OPP, off, n)
            f_copy(h, i).start()

    def near(i):
        for h in range(2):
            off, n = piece(h, i)
            send_n[pl.ds(off, n), :] = part_sum(RIGHT if h == 0 else LEFT, off, n)
            n_copy(h, i).start()

    def relay(i):
        for h in range(2):
            off, n = piece(h, i)
            mine = part_sum(LEFT if h == 0 else RIGHT, off, n)
            f_copy(h, i).wait_recv()
            recv_f[pl.ds(off, n), :] = recv_f[pl.ds(off, n), :] + mine
            r_copy(h, i).start()

    def account(z, first):
        zr = z.reshape(z.shape[0] // 8, 8, rows)
        top = jnp.max(zr, axis=0)
        if first:
            m_acc[...] = top
            s_acc[...] = jnp.sum(jnp.exp(zr - top[None]), axis=0)
        else:
            old = m_acc[...]
            new = jnp.maximum(old, top)
            m_acc[...] = new
            s_acc[...] = s_acc[...] * jnp.exp(old - new) + jnp.sum(jnp.exp(zr - new[None]), axis=0)

    def arrive(h, i):
        (r_copy if h == 0 else n_copy)(h, i).wait_recv()
        (n_copy if h == 0 else r_copy)(h, i).wait_recv()

    def settle(i):
        if isinstance(i, int) and i == 0:
            arrive(0, 0)
            arrive(1, 0)
            for off in range(tail0, n_block, CHUNK):
                n = min(CHUNK, n_block - off)
                z = part_sum(OWN, off, n) + recv_l[off:off + n, :] + recv_r[off:off + n, :]
                account(z, off == tail0)
                logits_ref[off:off + n, :] = z
            return
        for h in range(2):
            off, n = piece(h, i)
            mine = part_sum(OWN, off, n)
            arrive(h, i)
            z = mine + recv_l[pl.ds(off, n), :] + recv_r[pl.ds(off, n), :]
            account(z, False)
            logits_ref[pl.ds(off, n), :] = z

    tok = jnp.broadcast_to(tok_ref[...], (128, rows)).T

    def gather(step):
        for other in range(2):
            blk_chip = lax.rem(chip + jnp.where(step == 0, STEP_OF_SLOT[0], jnp.where(
                step == 1, STEP_OF_SLOT[1], jnp.where(step == 2, STEP_OF_SLOT[2], STEP_OF_SLOT[3]))), n_chip)
            blk = blk_chip * 2 + (1 - core if other else core)
            base = vp * (n_tp * n_block) + blk * n_block
            ref = e_oth if other else e_own
            acc = pick[...]
            for off in range(0, n_block, 512):
                n = min(512, n_block - off)
                for o, k in ((off, n // 128 * 128), (off + n // 128 * 128, n % 128)):
                    if k == 0:
                        continue
                    lane = lax.broadcasted_iota(jnp.int32, (rows, k), 1) + (base + o)
                    if k % 128 == 0:
                        want = jnp.concatenate([tok] * (k // 128), axis=1) if k > 128 else tok
                    else:
                        want = tok[:, :k]
                    hot = jnp.where(want == lane, 1.0, 0.0).astype(BF16)
                    acc = acc + jnp.dot(hot, ref[step, o:o + k, :], preferred_element_type=F32)
            pick[...] = acc

    def v_copy(src_buf, src_idx, dst_buf, stage, j, peer):
        return pltpu.make_async_remote_copy(
            src_ref=src_buf.at[src_idx] if src_idx is not None else src_buf, dst_ref=dst_buf,
            send_sem=v_send.at[stage, j], recv_sem=v_recv.at[stage, j],
            device_id={"vp": peer}, device_id_type=MESH)

    def rs_copy(j):
        peer = lax.rem(vp + j, n_vp)
        return v_copy(pick.at[pl.ds(pl.multiple_of(peer * slab, 8), slab), :], None, rs_buf.at[vp], 0, j, peer)

    def rs_in(j):
        src = lax.rem(vp + n_vp - j, n_vp)
        return v_copy(rs_buf, src, rs_buf.at[src], 0, j, src)

    def vp_copy(buf, stage, j):
        peer = lax.rem(vp + j, n_vp)
        return v_copy(buf, vp, buf.at[vp], stage, j, peer)

    def vp_in(buf, stage, j):
        src = lax.rem(vp + n_vp - j, n_vp)
        return v_copy(buf, src, buf.at[src], stage, j, src)

    def rows_scatter():
        for j in range(1, n_vp):
            rs_copy(j).start()
        rs_buf[vp] = pick[pl.ds(pl.multiple_of(vp * slab, 8), slab), :]

    def rows_stats():
        for j in range(1, n_vp):
            rs_in(j).wait_recv()
        tot = rs_buf[0]
        for j in range(1, n_vp):
            tot = tot + rs_buf[j]
        ag_buf[vp] = tot
        lane = lax.broadcasted_iota(jnp.int32, (slab, 128), 1)
        row_st[tp] = jnp.where(lane == 0, jnp.sum(tot, axis=1, keepdims=True), jnp.sum(tot * tot, axis=1, keepdims=True))
        tp_start(row_st, 1)

    def rows_norm():
        tp_wait(row_st, 1)
        tot = row_st[0]
        for j in range(1, n_tp):
            tot = tot + row_st[j]
        mu = tot[:, 0:1] / full_width
        rs = lax.rsqrt(tot[:, 1:2] / full_width - mu * mu + NORM_EPS)
        out = ((ag_buf[vp] - mu) * rs * eg_ref[...] + eb_ref[...]).astype(BF16)
        ag_buf[vp] = out.astype(F32)
        for j in range(1, n_vp):
            vp_copy(ag_buf, 1, j).start()

    def rows_out():
        for j in range(1, n_vp):
            vp_in(ag_buf, 1, j).wait_recv()
        for j in range(n_vp):
            next_ref[j * slab:(j + 1) * slab, :] = ag_buf[j]

    pick[...] = jnp.zeros_like(pick)

    load(OPP, False).wait()
    for q in range(2):
        ex_copy(OPP, q).wait_recv()
        far(q)
    for slot in (LEFT, RIGHT):
        load(slot, False).wait()
        for q in range(2):
            ex_copy(slot, q).wait_recv()
    near(0)
    far(2)
    relay(0)
    load(OWN, False).wait()
    for q in range(2):
        ex_copy(OWN, q).wait_recv()

    def round_body(i, carry):
        near(i)

        @pl.when(i + 2 < n_round)
        def _():
            far(i + 2)

        relay(i)

        @pl.when(i <= 4)
        def _():
            gather(i - 1)

        @pl.when(i == 5)
        def _():
            rows_scatter()

        @pl.when(i == 6)
        def _():
            rows_stats()

        @pl.when(i == 7)
        def _():
            rows_norm()

        @pl.when(i == 2)
        def _():
            settle(0)

        @pl.when(i >= 3)
        def _():
            settle(i - 2)

        return carry

    lax.fori_loop(1, n_round, round_body, 0)

    rows_out()

    def last_body(i, carry):
        settle(i)
        return carry

    lax.fori_loop(n_round - 2, n_round, last_body, 0)

    def merge(buf, n):
        top = buf[0, 0:1]
        for j in range(1, n):
            top = jnp.maximum(top, buf[j, 0:1])
        tot = buf[0, 1:2] * jnp.exp(buf[0, 0:1] - top)
        for j in range(1, n):
            tot = tot + buf[j, 1:2] * jnp.exp(buf[j, 0:1] - top)
        return top, tot

    m8 = m_acc[...]
    top = jnp.max(m8, axis=0, keepdims=True)
    tot = jnp.sum(s_acc[...] * jnp.exp(m8 - top), axis=0, keepdims=True)
    st_lse[tp] = jnp.where(sub8 == 0, top, tot)
    tp_start(st_lse, 2)
    tp_wait(st_lse, 2)
    top, tot = merge(st_lse, n_tp)
    st_all[vp] = jnp.where(sub8 == 0, top, tot)
    for j in range(1, n_vp):
        vp_copy(st_all, 2, j).start()
    hx_copy.wait_send()
    for slot in range(4):
        for q in range(2):
            ex_copy(slot, q).wait_send()
    for h in range(2):
        f_copy(h, 0).wait_send()
        n_copy(h, 0).wait_send()
        r_copy(h, 0).wait_send()

    def drain(i, carry):
        for h in range(2):
            f_copy(h, i).wait_send()
            n_copy(h, i).wait_send()
            r_copy(h, i).wait_send()
        return carry

    lax.fori_loop(1, n_round, drain, 0)
    tp_drain(st_ln, 0)
    tp_drain(row_st, 1)
    tp_drain(st_lse, 2)
    for j in range(1, n_vp):
        rs_copy(j).wait_send()
        vp_copy(ag_buf, 1, j).wait_send()
    for j in range(1, n_vp):
        vp_in(st_all, 2, j).wait_recv()
    top, tot = merge(st_all, n_vp)
    lse_ref[...] = top + jnp.log(tot)
    for j in range(1, n_vp):
        vp_copy(st_all, 2, j).wait_send()


def solution(mesh):
    n_vp, n_tp = mesh.shape["vp"], mesh.shape["tp"]

    def per_device(hidden, lnf_gain, lnf_bias, emb_table, next_tok, eln_gain, eln_bias):
        rows, width = hidden.shape
        n_block = emb_table.shape[0] // n_tp
        slab = rows // n_vp
        n_round = n_block // 2 // CHUNK + 1
        dma = pltpu.SemaphoreType.DMA
        vmem = pl.BlockSpec(memory_space=pltpu.VMEM)
        logits, lse, next_in = pl.pallas_call(
            functools.partial(head_kernel, n_vp, n_tp, n_block, width * n_tp),
            out_shape=(
                jax.ShapeDtypeStruct((n_block, rows), F32),
                jax.ShapeDtypeStruct((1, rows), F32),
                jax.ShapeDtypeStruct((rows, width), F32),
            ),
            in_specs=[vmem, vmem, vmem, pl.BlockSpec(memory_space=pl.ANY), vmem, vmem, vmem],
            out_specs=(vmem, vmem, vmem),
            scratch_shapes=[
                pltpu.VMEM((4, n_block, width), BF16),
                pltpu.VMEM((4, n_block, width), BF16),
                pltpu.VMEM((4, n_block, width), F32),
                pltpu.VMEM((4, n_block, width), F32),
                pltpu.VMEM((n_block, rows), F32),
                pltpu.VMEM((n_block, rows), F32),
                pltpu.VMEM((n_block, rows), F32),
                pltpu.VMEM((n_block, rows), F32),
                pltpu.VMEM((n_block, rows), F32),
                pltpu.VMEM((2, width, rows + 256), F32),
                pltpu.VMEM((2, width, rows), BF16),
                pltpu.VMEM((8, rows), F32),
                pltpu.VMEM((8, rows), F32),
                pltpu.VMEM((rows, width), F32),
                pltpu.VMEM((n_tp, 8, rows), F32),
                pltpu.VMEM((n_tp, 8, rows), F32),
                pltpu.VMEM((n_vp, 8, rows), F32),
                pltpu.VMEM((n_vp, slab, width), F32),
                pltpu.VMEM((n_tp, slab, 128), F32),
                pltpu.VMEM((n_vp, slab, width), F32),
                dma((4,)), dma((4,)), dma((4, 2)), dma((4, 2)), dma((1,)), dma((1,)),
                dma((2, n_round)), dma((2, n_round)), dma((2, n_round)), dma((2, n_round)), dma((2, n_round)), dma((2, n_round)),
                dma((3, n_tp)), dma((3, n_tp)), dma((3, n_vp)), dma((3, n_vp)),
            ],
            compiler_params=pltpu.CompilerParams(
                collective_id=0, has_side_effects=True, vmem_limit_bytes=62 * 1024 * 1024),
            cost_estimate=pl.CostEstimate(
                flops=4 * rows * n_block * n_tp * width, bytes_accessed=16 * n_block * n_tp * width, transcendentals=rows * n_block),
        )(hidden, lnf_gain[None, :], lnf_bias[None, :], emb_table, next_tok[None, :], eln_gain[None, :], eln_bias[None, :])
        return (logits - lse).T, lse[0], next_in.astype(BF16)

    return jax.shard_map(
        per_device,
        mesh=mesh,
        in_specs=(P("dp", "tp"), P("tp"), P("tp"), P("vp", "tp"), P("dp"), P("tp"), P("tp")),
        out_specs=(P("dp", ("vp", "tp")), P("dp"), P("dp", "tp")),
        check_vma=False,
    )
```

time: 441 us -> 168 us (0.38)
  waiting for transfers between devices: 245 us -> 0 us
  Pallas kernels: 0 us -> 162 us
  blocking collectives: 143 us -> 0 us
  matrix products: 16.3 us -> 0 us
  between operations: 14.2 us -> 0.66 us
  other arithmetic: 14.9 us -> 5.37 us
  local copies, waits for them, and re-layouts: 6.9 us -> 0.59 us
    pallas_call x0 -> x1, Pallas kernels: none -> 162 us  [per_device(): pl.pallas_call(functools.partial(head_kernel, n_vp, n_tp, n_block, width...]
    reduce_scatter x1 -> x0, waiting for transfers between devices: 159 us -> none  [per_device(): lax.psum_scatter(shard_logits, 'tp', scatter_dimension=1, tiled=True)]
    psum x1 -> x0, waiting for transfers between devices: 85.9 us -> none  [per_device(): tok_rows = lax.psum(picked, 'vp')]
    psum x2 -> x0, blocking collectives: 77.5 us -> none  [the longest x1 63.1 us: global_lse(): lax.psum(jnp.sum(jnp.exp(logits - row_top[:, None]), axis=1), ('vp', 'tp'))]
    pmax x1 -> x0, blocking collectives: 65.7 us -> none  [global_lse(): row_top = lax.pmax(jnp.max(logits, axis=1), ('vp', 'tp'))]
    dot_general x1 -> x0, matrix products: 16.3 us -> none  [per_device(): lax.dot_general(normed, emb_table, (((1,), (1,)), ((), ())), preferred_el...]
    gather x1 -> x0, local copies, waits for them, and re-layouts: 5.87 us -> none  [per_device(): jnp.take(emb_table, jnp.clip(local_idx, 0, block_rows - 1), axis=0)]
    reduce_sum x3 -> x0, other arithmetic: 5.17 us -> none  [the longest x1 2.74 us: global_lse(): jnp.sum(jnp.exp(logits - row_top[:, None]), axis=1)]
  transfers between devices with their start and end apart: 2 -> 0, of which waited for: 2 -> 0; matrix products, arithmetic and copies ran while one was open for 0% -> 0% of each run, Pallas kernels for 0% -> 0%
where the time goes in v1:
time: 168 us
  Pallas kernels  162 us (96%)
  other arithmetic  5.37 us (3%)
    pallas_call x1, Pallas kernels, per_device(): pl.pallas_call(functools.partial(head_kernel, n_vp, n_tp, n_block, width...  162 us
    transpose x1, other arithmetic, per_device(): return ((logits - lse).T, lse[0], next_in.astype(BF16))  4.64 us

profile of v1, /device:TPU:1, one launch (start us, length us, event | category | flops | bytes accessed | tf_op | source)
XLA Modules:
  0.0 168.2 jit_solution(3067269327169752930)
XLA Ops:
  0.6 161.6 %shard_map.94 = (f32[1960,512]{1,0:T(8,128)}, f32[1,512]{1,0:T(1,128)}, f32[512,256]{1,0:T(8,128)}) custom-call(bf16[512,256]{1,0:T(8,128)(2,1)} %hid_ref.1, f32[1,256]{1,0:T(1,128)} %bitcast.11, f32[1,256]{1,0:T(1,128)} %bitcast.12, bf16[15680,256]{1,0:T(8,128)(2,1)} %emb_ref.1, s32[1,512]{1,0:T(1,128)} %bitcast.10, f32[1,256]{1,0:T(1,128)} %bitcast.13, ...), custom_call_target="tpu_custom_call" | custom-call | flops 8220835840 | bytes 64225280 | tf_op jit(solution)/shard_map/pallas_call | solution.py:423
  162.2 0.0 copy-start
  162.2 0.0 copy-start.1
  162.2 4.6 %subtract_bitcast_fusion = f32[512,1960]{0,1:T(8,128)} fusion(f32[1960,512]{1,0:T(8,128)} %get-tuple-element.6, f32[512]{0:T(512)} %bitcast.8), kind=kLoop, calls=%fused_computation | loop fusion | flops 1003520 | bytes 8030208 | tf_op jit(solution)/shard_map/transpose | solution.py:462
  166.9 0.0 copy-done
  166.9 0.7 convert_element_type.3
  167.6 0.0 copy-done.1
  167.6 0.6 copy.11
Async XLA Ops:
  162.2 4.7 %copy-start = (f32[512,256]{1,0:T(8,128)S(1)}, f32[512,256]{1,0:T(8,128)}, u32[]{:S(2)}) copy-start(f32[512,256]{1,0:T(8,128)} %get-tuple-element.8) | copy-start | bytes 1572868
  162.2 5.4 %copy-start.1 = (f32[1,512]{1,0:T(1,128)S(1)}, f32[1,512]{1,0:T(1,128)}, u32[]{:S(2)}) copy-start(f32[1,512]{1,0:T(1,128)} %get-tuple-element.7) | copy-start | bytes 6148

commit v2 on v1

--- a/solution.py
+++ b/solution.py
@@ -69,8 +69,8 @@
     hx[0, :, 0:rows] = h_t
     hx[0, :, rows:rows + 128] = jnp.broadcast_to(g_ref[...], (128, width)).T
     hx[0, :, rows + 128:rows + 256] = jnp.broadcast_to(b_ref[...], (128, width)).T
-    sub8 = lax.broadcasted_iota(jnp.int32, (8, rows), 0)
-    st_ln[tp] = jnp.where(sub8 == 0, jnp.sum(h_t, axis=0, keepdims=True), jnp.sum(h_t * h_t, axis=0, keepdims=True))
+    st_ln[tp, :, 0:rows] = jnp.sum(h_t, axis=0, keepdims=True)
+    st_ln[tp, :, rows:2 * rows] = jnp.sum(h_t * h_t, axis=0, keepdims=True)
 
     pl.semaphore_wait(barrier, n_tp + n_vp - 2)
 
@@ -121,8 +121,8 @@
     total = st_ln[0]
     for j in range(1, n_tp):
         total = total + st_ln[j]
-    mean = total[0:1] / full_width
-    rstd = lax.rsqrt(total[1:2] / full_width - mean * mean + NORM_EPS)
+    mean = total[:, 0:rows] / full_width
+    rstd = lax.rsqrt(total[:, rows:2 * rows] / full_width - mean * mean + NORM_EPS)
 
     def norm(which):
         gain = hx[which, :, rows:rows + 128]
@@ -324,20 +324,21 @@
 
         relay(i)
 
-        @pl.when(i <= 4)
-        def _():
-            gather(i - 1)
-
-        @pl.when(i == 5)
+        @pl.when(i <= 2)
+        def _():
+            gather(2 * i - 2)
+            gather(2 * i - 1)
+
+        @pl.when(i == 3)
         def _():
             rows_scatter()
 
+        @pl.when(i == 4)
+        def _():
+            rows_stats()
+
         @pl.when(i == 6)
         def _():
-            rows_stats()
-
-        @pl.when(i == 7)
-        def _():
             rows_norm()
 
         @pl.when(i == 2)
@@ -351,8 +352,6 @@
         return carry
 
     lax.fori_loop(1, n_round, round_body, 0)
-
-    rows_out()
 
     def last_body(i, carry):
         settle(i)
@@ -361,24 +360,23 @@
     lax.fori_loop(n_round - 2, n_round, last_body, 0)
 
     def merge(buf, n):
-        top = buf[0, 0:1]
+        top = buf[0]
         for j in range(1, n):
-            top = jnp.maximum(top, buf[j, 0:1])
-        tot = buf[0, 1:2] * jnp.exp(buf[0, 0:1] - top)
+            top = jnp.maximum(top, buf[j])
+        tot = jnp.exp(buf[0] - top)
         for j in range(1, n):
-            tot = tot + buf[j, 1:2] * jnp.exp(buf[j, 0:1] - top)
-        return top, tot
+            tot = tot + jnp.exp(buf[j] - top)
+        return top + jnp.log(tot)
 
     m8 = m_acc[...]
     top = jnp.max(m8, axis=0, keepdims=True)
-    tot = jnp.sum(s_acc[...] * jnp.exp(m8 - top), axis=0, keepdims=True)
-    st_lse[tp] = jnp.where(sub8 == 0, top, tot)
+    st_lse[tp] = top + jnp.log(jnp.sum(s_acc[...] * jnp.exp(m8 - top), axis=0, keepdims=True))
     tp_start(st_lse, 2)
     tp_wait(st_lse, 2)
-    top, tot = merge(st_lse, n_tp)
-    st_all[vp] = jnp.where(sub8 == 0, top, tot)
+    st_all[vp] = merge(st_lse, n_tp)
     for j in range(1, n_vp):
         vp_copy(st_all, 2, j).start()
+    rows_out()
     hx_copy.wait_send()
     for slot in range(4):
         for q in range(2):
@@ -404,10 +402,26 @@
         vp_copy(ag_buf, 1, j).wait_send()
     for j in range(1, n_vp):
         vp_in(st_all, 2, j).wait_recv()
-    top, tot = merge(st_all, n_vp)
-    lse_ref[...] = top + jnp.log(tot)
+    lse_ref[...] = merge(st_all, n_vp)
     for j in range(1, n_vp):
         vp_copy(st_all, 2, j).wait_send()
+
+
+def finish_kernel(n_piece, z_ref, lse_ref, next_ref, out_ref, sum_ref, row_ref, buf, sems):
+    lse = lse_ref[...]
+    n = z_ref.shape[0] // n_piece
+
+    def put(j):
+        part = pl.ds(j * n, n)
+        return pltpu.make_async_copy(buf.at[part, :], out_ref.at[part, :], sems.at[j])
+
+    for j in range(n_piece):
+        buf[j * n:(j + 1) * n, :] = z_ref[j * n:(j + 1) * n, :] - lse
+        put(j).start()
+    sum_ref[...] = lse
+    row_ref[...] = next_ref[...].astype(BF16)
+    for j in range(n_piece):
+        put(j).wait()
 
 
 def solution(mesh):
@@ -423,9 +437,9 @@
         logits, lse, next_in = pl.pallas_call(
             functools.partial(head_kernel, n_vp, n_tp, n_block, width * n_tp),
             out_shape=(
-                jax.ShapeDtypeStruct((n_block, rows), F32),
-                jax.ShapeDtypeStruct((1, rows), F32),
-                jax.ShapeDtypeStruct((rows, width), F32),
+                pltpu.VMEM((n_block, rows), F32),
+                pltpu.VMEM((1, rows), F32),
+                pltpu.VMEM((rows, width), F32),
             ),
             in_specs=[vmem, vmem, vmem, pl.BlockSpec(memory_space=pl.ANY), vmem, vmem, vmem],
             out_specs=(vmem, vmem, vmem),
@@ -444,9 +458,9 @@
                 pltpu.VMEM((8, rows), F32),
                 pltpu.VMEM((8, rows), F32),
                 pltpu.VMEM((rows, width), F32),
-                pltpu.VMEM((n_tp, 8, rows), F32),
-                pltpu.VMEM((n_tp, 8, rows), F32),
-                pltpu.VMEM((n_vp, 8, rows), F32),
+                pltpu.VMEM((n_tp, 1, 2 * rows), F32),
+                pltpu.VMEM((n_tp, 1, rows), F32),
+                pltpu.VMEM((n_vp, 1, rows), F32),
                 pltpu.VMEM((n_vp, slab, width), F32),
                 pltpu.VMEM((n_tp, slab, 128), F32),
                 pltpu.VMEM((n_vp, slab, width), F32),
@@ -455,11 +469,24 @@
                 dma((3, n_tp)), dma((3, n_tp)), dma((3, n_vp)), dma((3, n_vp)),
             ],
             compiler_params=pltpu.CompilerParams(
-                collective_id=0, has_side_effects=True, vmem_limit_bytes=62 * 1024 * 1024),
+                collective_id=0, has_side_effects=True, vmem_limit_bytes=53 * 1024 * 1024),
             cost_estimate=pl.CostEstimate(
                 flops=4 * rows * n_block * n_tp * width, bytes_accessed=16 * n_block * n_tp * width, transcendentals=rows * n_block),
         )(hidden, lnf_gain[None, :], lnf_bias[None, :], emb_table, next_tok[None, :], eln_gain[None, :], eln_bias[None, :])
-        return (logits - lse).T, lse[0], next_in.astype(BF16)
+        n_piece = 5
+        logprobs_t, log_sum, next_bf = pl.pallas_call(
+            functools.partial(finish_kernel, n_piece),
+            out_shape=(
+                jax.ShapeDtypeStruct((n_block, rows), F32),
+                jax.ShapeDtypeStruct((1, rows), F32),
+                jax.ShapeDtypeStruct((rows, width), BF16),
+            ),
+            in_specs=[vmem, vmem, vmem],
+            out_specs=(pl.BlockSpec(memory_space=pl.ANY), vmem, vmem),
+            scratch_shapes=[pltpu.VMEM((n_block, rows), F32), dma((n_piece,))],
+            compiler_params=pltpu.CompilerParams(vmem_limit_bytes=16 * 1024 * 1024),
+        )(logits, lse, next_in)
+        return logprobs_t.T, log_sum[0], next_bf
 
     return jax.shard_map(
         per_device,

time: 168 us -> 160 us (0.952)
  other arithmetic: 5.37 us -> 0 us
  Pallas kernels: 162 us -> 159 us
    pallas_call x1, Pallas kernels: 162 us -> 156 us  [per_device(): pl.pallas_call(functools.partial(head_kernel, n_vp, n_tp, n_block, width...]
    transpose x1 -> x0, other arithmetic: 4.64 us -> none  [per_device(): return ((logits - lse).T, lse[0], next_in.astype(BF16))]
    pallas_call x0 -> x1, Pallas kernels: none -> 2.75 us  [per_device(): pl.pallas_call(functools.partial(finish_kernel, n_piece), out_shape=(jax....]
where the time goes in v2:
time: 160 us
  Pallas kernels  159 us (99%)
    pallas_call x1, Pallas kernels, per_device(): pl.pallas_call(functools.partial(head_kernel, n_vp, n_tp, n_block, width...  156 us

profile of v2, /device:TPU:1, one launch (start us, length us, event | category | flops | bytes accessed | tf_op | source)
XLA Modules:
  0.0 159.7 jit_solution(9814459430591515351)
XLA Ops:
  0.6 156.3 %shard_map.94 = (f32[1960,512]{1,0:T(8,128)S(1)}, f32[1,512]{1,0:T(1,128)S(1)}, f32[512,256]{1,0:T(8,128)S(1)}) custom-call(bf16[512,256]{1,0:T(8,128)(2,1)} %hid_ref.1, f32[1,256]{1,0:T(1,128)} %bitcast.10, f32[1,256]{1,0:T(1,128)} %bitcast.11, bf16[15680,256]{1,0:T(8,128)(2,1)} %emb_ref.1, s32[1,512]{1,0:T(1,128)} %bitcast.8, f32[1,256]{1,0:T(1,128)} %bitcast.12, ...), custom_call_target="tpu_custom_call" | custom-call | flops 8220835840 | bytes 64225280 | tf_op jit(solution)/shard_map/pallas_call | solution.py:437
  157.0 2.7 %shard_map.95 = (f32[1960,512]{1,0:T(8,128)}, f32[1,512]{1,0:T(1,128)}, bf16[512,256]{1,0:T(8,128)(2,1)}) custom-call(f32[1960,512]{1,0:T(8,128)S(1)} %get-tuple-element.9.z_ref, f32[1,512]{1,0:T(1,128)S(1)} %get-tuple-element.10.lse_ref, f32[512,256]{1,0:T(8,128)S(1)} %get-tuple-element.11.next_ref), custom_call_target="tpu_custom_call" | custom-call | tf_op jit(solution)/shard_map/pallas_call | solution.py:477

commit v3 on v2

--- a/solution.py
+++ b/solution.py
@@ -18,20 +18,20 @@
 
 
 def head_kernel(n_vp, n_tp, n_block, full_width,
-                hid_ref, g_ref, b_ref, emb_ref, tok_ref, eg_ref, eb_ref,
+                hid_hbm, g_hbm, b_hbm, emb_ref, tok_hbm, eg_hbm, eb_hbm,
                 logits_ref, lse_ref, next_ref,
                 e_own, e_oth, e_out, e_in, send_f, recv_f, send_n, recv_l, recv_r,
                 hx, xn, m_acc, s_acc, pick, st_ln, st_lse, st_all, rs_buf, row_st, ag_buf,
                 own_sem, oth_sem, ex_send, ex_recv, hx_send, hx_recv,
                 f_send, f_recv, n_send, r_send, l_recv, r_recv,
-                t_send, t_recv, v_send, v_recv):
+                t_send, t_recv, v_send, v_recv,
+                hid_ref, g_ref, b_ref, tok_ref, eg_ref, eb_ref, in_sem):
     vp = lax.axis_index("vp")
     tp = lax.axis_index("tp")
     core = lax.rem(tp, 2)
     chip = tp // 2
     n_chip = n_tp // 2
-    rows = hid_ref.shape[0]
-    width = hid_ref.shape[1]
+    rows, width = hid_hbm.shape
     slab = rows // n_vp
     left = {"tp": lax.rem(chip + n_chip - 1, n_chip) * 2 + core}
     right = {"tp": lax.rem(chip + 1, n_chip) * 2 + core}
@@ -55,9 +55,8 @@
         dst = (e_oth if other else e_own).at[slot]
         return pltpu.make_async_copy(src, dst, (oth_sem if other else own_sem).at[slot])
 
-    for slot in range(4):
-        load(slot, True).start()
-        load(slot, False).start()
+    small_in = [pltpu.make_async_copy(src, dst, in_sem.at[k]) for k, (src, dst) in enumerate((
+        (hid_hbm, hid_ref), (g_hbm, g_ref), (b_hbm, b_ref), (tok_hbm, tok_ref), (eg_hbm, eg_ref), (eb_hbm, eb_ref)))]
 
     barrier = pltpu.get_barrier_semaphore()
     for j in range(1, n_tp):
@@ -65,6 +64,16 @@
     for j in range(1, n_vp):
         pl.semaphore_signal(barrier, inc=1, device_id={"vp": lax.rem(vp + j, n_vp)}, device_id_type=MESH)
 
+    for copy in small_in[:3]:
+        copy.start()
+    for slot in range(4):
+        load(slot, True).start()
+        load(slot, False).start()
+    for copy in small_in[3:]:
+        copy.start()
+
+    for copy in small_in[:3]:
+        copy.wait()
     h_t = hid_ref[...].astype(F32).T
     hx[0, :, 0:rows] = h_t
     hx[0, :, rows:rows + 128] = jnp.broadcast_to(g_ref[...], (128, width)).T
@@ -210,14 +219,16 @@
                 account(z, off == tail0)
                 logits_ref[off:off + n, :] = z
             return
+        mine = [part_sum(OWN, *piece(h, i)) for h in range(2)]
         for h in range(2):
             off, n = piece(h, i)
-            mine = part_sum(OWN, off, n)
             arrive(h, i)
-            z = mine + recv_l[pl.ds(off, n), :] + recv_r[pl.ds(off, n), :]
+            z = mine[h] + recv_l[pl.ds(off, n), :] + recv_r[pl.ds(off, n), :]
             account(z, False)
             logits_ref[pl.ds(off, n), :] = z
 
+    for copy in small_in[3:]:
+        copy.wait()
     tok = jnp.broadcast_to(tok_ref[...], (128, rows)).T
 
     def gather(step):
@@ -277,7 +288,10 @@
             tot = tot + rs_buf[j]
         ag_buf[vp] = tot
         lane = lax.broadcasted_iota(jnp.int32, (slab, 128), 1)
-        row_st[tp] = jnp.where(lane == 0, jnp.sum(tot, axis=1, keepdims=True), jnp.sum(tot * tot, axis=1, keepdims=True))
+        both = jnp.where(lane == 0, jnp.sum(tot, axis=1, keepdims=True), jnp.sum(tot * tot, axis=1, keepdims=True)).T
+        row_st[tp] = jnp.zeros((1, 256), F32)
+        row_st[tp, :, 0:slab] = both[0:1]
+        row_st[tp, :, 128:128 + slab] = both[1:2]
         tp_start(row_st, 1)
 
     def rows_norm():
@@ -285,8 +299,10 @@
         tot = row_st[0]
         for j in range(1, n_tp):
             tot = tot + row_st[j]
-        mu = tot[:, 0:1] / full_width
-        rs = lax.rsqrt(tot[:, 1:2] / full_width - mu * mu + NORM_EPS)
+        mu = tot[:, 0:128] / full_width
+        rs = lax.rsqrt(tot[:, 128:256] / full_width - mu * mu + NORM_EPS)
+        mu = jnp.broadcast_to(mu, (128, 128)).T[0:slab, 0:1]
+        rs = jnp.broadcast_to(rs, (128, 128)).T[0:slab, 0:1]
         out = ((ag_buf[vp] - mu) * rs * eg_ref[...] + eb_ref[...]).astype(BF16)
         ag_buf[vp] = out.astype(F32)
         for j in range(1, n_vp):
@@ -370,10 +386,7 @@
 
     m8 = m_acc[...]
     top = jnp.max(m8, axis=0, keepdims=True)
-    st_lse[tp] = top + jnp.log(jnp.sum(s_acc[...] * jnp.exp(m8 - top), axis=0, keepdims=True))
-    tp_start(st_lse, 2)
-    tp_wait(st_lse, 2)
-    st_all[vp] = merge(st_lse, n_tp)
+    st_all[vp] = top + jnp.log(jnp.sum(s_acc[...] * jnp.exp(m8 - top), axis=0, keepdims=True))
     for j in range(1, n_vp):
         vp_copy(st_all, 2, j).start()
     rows_out()
@@ -396,15 +409,18 @@
     lax.fori_loop(1, n_round, drain, 0)
     tp_drain(st_ln, 0)
     tp_drain(row_st, 1)
-    tp_drain(st_lse, 2)
     for j in range(1, n_vp):
         rs_copy(j).wait_send()
         vp_copy(ag_buf, 1, j).wait_send()
     for j in range(1, n_vp):
         vp_in(st_all, 2, j).wait_recv()
-    lse_ref[...] = merge(st_all, n_vp)
+    st_lse[tp] = merge(st_all, n_vp)
+    tp_start(st_lse, 2)
     for j in range(1, n_vp):
         vp_copy(st_all, 2, j).wait_send()
+    tp_wait(st_lse, 2)
+    lse_ref[...] = merge(st_lse, n_tp)
+    tp_drain(st_lse, 2)
 
 
 def finish_kernel(n_piece, z_ref, lse_ref, next_ref, out_ref, sum_ref, row_ref, buf, sems):
@@ -441,7 +457,7 @@
                 pltpu.VMEM((1, rows), F32),
                 pltpu.VMEM((rows, width), F32),
             ),
-            in_specs=[vmem, vmem, vmem, pl.BlockSpec(memory_space=pl.ANY), vmem, vmem, vmem],
+            in_specs=[pl.BlockSpec(memory_space=pl.ANY)] * 7,
             out_specs=(vmem, vmem, vmem),
             scratch_shapes=[
                 pltpu.VMEM((4, n_block, width), BF16),
@@ -462,11 +478,18 @@
                 pltpu.VMEM((n_tp, 1, rows), F32),
                 pltpu.VMEM((n_vp, 1, rows), F32),
                 pltpu.VMEM((n_vp, slab, width), F32),
-                pltpu.VMEM((n_tp, slab, 128), F32),
+                pltpu.VMEM((n_tp, 1, 256), F32),
                 pltpu.VMEM((n_vp, slab, width), F32),
                 dma((4,)), dma((4,)), dma((4, 2)), dma((4, 2)), dma((1,)), dma((1,)),
                 dma((2, n_round)), dma((2, n_round)), dma((2, n_round)), dma((2, n_round)), dma((2, n_round)), dma((2, n_round)),
                 dma((3, n_tp)), dma((3, n_tp)), dma((3, n_vp)), dma((3, n_vp)),
+                pltpu.VMEM((rows, width), BF16),
+                pltpu.VMEM((1, width), F32),
+                pltpu.VMEM((1, width), F32),
+                pltpu.VMEM((1, rows), jnp.int32),
+                pltpu.VMEM((1, width), F32),
+                pltpu.VMEM((1, width), F32),
+                dma((6,)),
             ],
             compiler_params=pltpu.CompilerParams(
                 collective_id=0, has_side_effects=True, vmem_limit_bytes=53 * 1024 * 1024),

time: 160 us -> 158 us (0.988)
  no operation moved by 1% of the time
where the time goes in v3:
time: 158 us
  Pallas kernels  158 us (100%)
    pallas_call x1, Pallas kernels, per_device(): pl.pallas_call(functools.partial(head_kernel, n_vp, n_tp, n_block, width...  155 us

profile of v3, /device:TPU:1, one launch (start us, length us, event | category | flops | bytes accessed | tf_op | source)
XLA Modules:
  0.0 158.2 jit_solution(4664919606253453100)
XLA Ops:
  0.6 154.8 %shard_map.94 = (f32[1960,512]{1,0:T(8,128)S(1)}, f32[1,512]{1,0:T(1,128)S(1)}, f32[512,256]{1,0:T(8,128)S(1)}) custom-call(bf16[512,256]{1,0:T(8,128)(2,1)} %hid_hbm.1, f32[1,256]{1,0:T(1,128)} %bitcast.10, f32[1,256]{1,0:T(1,128)} %bitcast.11, bf16[15680,256]{1,0:T(8,128)(2,1)} %emb_ref.1, s32[1,512]{1,0:T(1,128)} %bitcast.8, f32[1,256]{1,0:T(1,128)} %bitcast.12, ...), custom_call_target="tpu_custom_call" | custom-call | flops 8220835840 | bytes 64225280 | tf_op jit(solution)/shard_map/pallas_call | solution.py:453
  155.5 2.7 %shard_map.95 = (f32[1960,512]{1,0:T(8,128)}, f32[1,512]{1,0:T(1,128)}, bf16[512,256]{1,0:T(8,128)(2,1)}) custom-call(f32[1960,512]{1,0:T(8,128)S(1)} %get-tuple-element.9.z_ref, f32[1,512]{1,0:T(1,128)S(1)} %get-tuple-element.10.lse_ref, f32[512,256]{1,0:T(8,128)S(1)} %get-tuple-element.11.next_ref), custom_call_target="tpu_custom_call" | custom-call | tf_op jit(solution)/shard_map/pallas_call | solution.py:500

commit v4 on v3

v4 whole, which is shorter than its diff:
```python
import functools

import jax
import jax.numpy as jnp
from jax import lax
from jax.experimental import pallas as pl
from jax.experimental.pallas import tpu as pltpu
from jax.sharding import PartitionSpec as P

NORM_EPS = 1e-5
MESH = pl.DeviceIdType.MESH
CHUNK = 128
F32 = jnp.float32
BF16 = jnp.bfloat16

OPP, LEFT, RIGHT, OWN = 0, 1, 2, 3
SIDE = 4
STEP_OF_SLOT = (2, 3, 1, 0)


def head_kernel(n_vp, n_tp, n_block, full_width,
                hid_hbm, g_hbm, b_hbm, emb_ref, tok_hbm, eg_hbm, eb_hbm,
                logits_ref, lse_ref, next_ref,
                e_own, e_oth, e_out, e_in, send_f, recv_f, send_n, recv_l, recv_r,
                hx, xn, m_acc, s_acc, pick, st_ln, st_lse, st_all, rs_buf, row_st, ag_buf,
                raw_src, raw_l, raw_r, slab_src, nb, nb_par, xnb,
                ld_sem, ex_send, ex_recv, hx_send, hx_recv,
                f_send, f_recv, n_send, r_send, l_recv, r_recv,
                t_send, t_recv, v_send, v_recv, raw_send, raw_recv, sx_send, sx_recv, nb_send, nb_recv, hop,
                hid_ref, g_ref, b_ref, tok_ref, eg_ref, eb_ref, in_sem):
    vp = lax.axis_index("vp")
    tp = lax.axis_index("tp")
    core = lax.rem(tp, 2)
    chip = tp // 2
    n_chip = n_tp // 2
    rows, width = hid_hbm.shape
    slab = rows // n_vp
    xslab = width // n_vp
    left_chip = lax.rem(chip + n_chip - 1, n_chip)
    right_chip = lax.rem(chip + 1, n_chip)
    left = {"tp": left_chip * 2 + core}
    right = {"tp": right_chip * 2 + core}
    partner = {"tp": chip * 2 + 1 - core}
    y = lax.rem(vp, SIDE)
    z = vp // SIDE
    n_z = n_vp // SIDE
    y_near = [{"vp": z * SIDE + lax.rem(y + d, SIDE)} for d in (1, SIDE - 1)]
    z_near = [{"vp": lax.rem(z + d, n_z) * SIDE + y} for d in (1, n_z - 1)]
    half = (n_block // 2) // CHUNK
    n_round = half + 1
    small = n_block - 2 * half * CHUNK
    small2 = (small // 16) * 8
    small1 = small - small2
    tail0 = 2 * half * CHUNK

    def piece(h, i):
        if isinstance(i, int) and i == 0:
            return (tail0 + small2, small1) if h == 0 else (tail0, small2)
        off = h * half * CHUNK + (i - 1) * CHUNK
        return (off if isinstance(i, int) else pl.multiple_of(off, CHUNK)), CHUNK

    barrier = pltpu.get_barrier_semaphore()
    for j in range(1, n_tp):
        pl.semaphore_signal(barrier, inc=1, device_id={"tp": lax.rem(tp + j, n_tp)}, device_id_type=MESH)
    for peer in y_near + z_near:
        pl.semaphore_signal(barrier, inc=1, device_id=peer, device_id_type=MESH)

    parts = ((tail0, small), (0, tail0))

    def load(slot, other, q):
        blk = lax.rem(chip + STEP_OF_SLOT[slot], n_chip) * 2 + (1 - core if other else core)
        off, n = parts[q]
        src = emb_ref.at[pl.ds(pl.multiple_of(blk * n_block + off, 8), n), :]
        dst = (e_oth if other else e_own).at[slot, pl.ds(off, n), :]
        return pltpu.make_async_copy(src, dst, ld_sem.at[int(other), slot, q])

    small_in = [pltpu.make_async_copy(src, dst, in_sem.at[k]) for k, (src, dst) in enumerate((
        (hid_hbm, hid_ref), (g_hbm, g_ref), (b_hbm, b_ref), (tok_hbm, tok_ref), (eg_hbm, eg_ref), (eb_hbm, eb_ref)))]
    for copy in small_in[:3]:
        copy.start()
    for slot in (RIGHT, LEFT):
        load(slot, True, 0).start()
        load(slot, False, 0).start()
    for slot, q in ((OPP, 0), (OPP, 1), (LEFT, 1), (RIGHT, 1), (OWN, 0), (OWN, 1)):
        load(slot, True, q).start()
        load(slot, False, q).start()
    for copy in small_in[3:]:
        copy.start()

    def total_recv(ref, sem):
        pltpu.make_async_remote_copy(src_ref=ref, dst_ref=ref, send_sem=sem, recv_sem=sem,
                                     device_id=partner, device_id_type=MESH).wait_recv()

    def total_send(ref, sem):
        pltpu.make_async_remote_copy(src_ref=ref, dst_ref=ref, send_sem=sem, recv_sem=sem,
                                     device_id=partner, device_id_type=MESH).wait_send()

    for copy in small_in[:3]:
        copy.wait()
    h_t = hid_ref[...].astype(F32).T
    hx[0, :, 0:rows] = h_t
    hx[0, :, rows:rows + 128] = jnp.broadcast_to(g_ref[...], (128, width)).T
    hx[0, :, rows + 128:rows + 256] = jnp.broadcast_to(b_ref[...], (128, width)).T
    st_ln[tp, :, 0:rows] = jnp.sum(h_t, axis=0, keepdims=True)
    st_ln[tp, :, rows:2 * rows] = jnp.sum(h_t * h_t, axis=0, keepdims=True)

    def convert(slot, q):
        off, n = parts[q]
        e_out[slot, off:off + n, :] = e_oth[slot, off:off + n, :].astype(F32)

    for slot in (RIGHT, LEFT):
        load(slot, True, 0).wait()
        load(slot, False, 0).wait()
        convert(slot, 0)
        off, n = piece(0 if slot == RIGHT else 1, 0)
        raw_src[off - tail0:off - tail0 + n, :] = e_own[slot, off:off + n, :].astype(F32)

    def raw_copy(slot, other):
        off, n = piece(0 if slot == RIGHT else 1, 0)
        src = e_out.at[slot, pl.ds(off, n), :] if other else raw_src.at[pl.ds(off - tail0, n), :]
        to = (right_chip if slot == RIGHT else left_chip) * 2 + (1 - core if other else core)
        return pltpu.make_async_remote_copy(
            src_ref=src, dst_ref=(raw_l if slot == RIGHT else raw_r).at[int(other)],
            send_sem=raw_send.at[int(slot == LEFT)], recv_sem=raw_recv.at[int(slot == LEFT)],
            device_id={"tp": to}, device_id_type=MESH)

    pl.semaphore_wait(barrier, n_tp + 3)

    def tp_start(buf, stage):
        for j in range(1, n_tp):
            pltpu.make_async_remote_copy(
                src_ref=buf.at[tp], dst_ref=buf.at[tp], send_sem=t_send.at[stage], recv_sem=t_recv.at[stage],
                device_id={"tp": lax.rem(tp + j, n_tp)}, device_id_type=MESH).start()

    def tp_wait(buf, stage):
        total_recv(buf.at[pl.ds(0, n_tp - 1)], t_recv.at[stage])

    def tp_drain(buf, stage):
        total_send(buf.at[pl.ds(0, n_tp - 1)], t_send.at[stage])

    tp_start(st_ln, 0)
    for other in (False, True):
        for slot in (RIGHT, LEFT):
            raw_copy(slot, other).start()

    hx_copy = pltpu.make_async_remote_copy(
        src_ref=hx.at[0], dst_ref=hx.at[1], send_sem=hx_send.at[0], recv_sem=hx_recv.at[0],
        device_id=partner, device_id_type=MESH)
    hx_copy.start()
    for peer in y_near:
        pl.semaphore_signal(hop.at[0], inc=1, device_id=peer, device_id_type=MESH)

    def ex_copy(slot, q):
        off, n = parts[q]
        return pltpu.make_async_remote_copy(
            src_ref=e_out.at[slot, pl.ds(off, n), :], dst_ref=e_in.at[slot, pl.ds(off, n), :],
            send_sem=ex_send.at[0], recv_sem=ex_recv.at[slot, q], device_id=partner, device_id_type=MESH)

    for slot, q in ((OPP, 0), (OPP, 1), (LEFT, 0), (RIGHT, 0), (LEFT, 1), (RIGHT, 1), (OWN, 0), (OWN, 1)):
        if q == 1 or slot in (OPP, OWN):
            load(slot, True, q).wait()
            convert(slot, q)
        ex_copy(slot, q).start()

    tp_wait(st_ln, 0)
    total = st_ln[0]
    for j in range(1, n_tp):
        total = total + st_ln[j]
    mean = total[:, 0:rows] / full_width
    rstd = lax.rsqrt(total[:, rows:2 * rows] / full_width - mean * mean + NORM_EPS)

    def norm(which):
        gain = hx[which, :, rows:rows + 128]
        bias = hx[which, :, rows + 128:rows + 256]
        for c in range(rows // 128):
            cols = slice(c * 128, c * 128 + 128)
            xn[which, :, cols] = ((hx[which, :, cols] - mean[:, cols]) * rstd[:, cols] * gain + bias).astype(BF16)

    def slab_copy(d):
        return pltpu.make_async_remote_copy(
            src_ref=slab_src, dst_ref=nb.at[d, pl.ds(pl.multiple_of(vp * xslab, 8), xslab), :],
            send_sem=sx_send.at[0], recv_sem=sx_recv.at[d], device_id=right if d == 0 else left, device_id_type=MESH)

    norm(0)
    slab_src[...] = xn[0, pl.ds(pl.multiple_of(vp * xslab, 8), xslab), :].astype(F32)
    for d in range(2):
        slab_copy(d).start()
    hx_copy.wait_recv()
    norm(1)

    def part_sum(slot, off, n):
        mine = e_own[slot, pl.ds(off, n), :]
        theirs = e_in[slot, pl.ds(off, n), :].astype(BF16)
        return (jnp.dot(mine, xn[0], preferred_element_type=F32)
                + jnp.dot(theirs, xn[1], preferred_element_type=F32))

    def f_copy(h, i):
        off, n = piece(h, i)
        return pltpu.make_async_remote_copy(
            src_ref=send_f.at[pl.ds(off, n), :], dst_ref=recv_f.at[pl.ds(off, n), :],
            send_sem=f_send.at[0], recv_sem=f_recv.at[h, i],
            device_id=left if h == 0 else right, device_id_type=MESH)

    def r_copy(h, i):
        off, n = piece(h, i)
        dst = (recv_r if h == 0 else recv_l).at[pl.ds(off, n), :]
        return pltpu.make_async_remote_copy(
            src_ref=recv_f.at[pl.ds(off, n), :], dst_ref=dst,
            send_sem=r_send.at[0], recv_sem=(r_recv if h == 0 else l_recv).at[h, i],
            device_id=left if h == 0 else right, device_id_type=MESH)

    def n_copy(h, i):
        off, n = piece(h, i)
        dst = (recv_l if h == 0 else recv_r).at[pl.ds(off, n), :]
        return pltpu.make_async_remote_copy(
            src_ref=send_n.at[pl.ds(off, n), :], dst_ref=dst,
            send_sem=n_send.at[0], recv_sem=(l_recv if h == 0 else r_recv).at[h, i],
            device_id=right if h == 0 else left, device_id_type=MESH)

    def far(i):
        for h in range(2):
            off, n = piece(h, i)
            send_f[pl.ds(off, n), :] = part_sum(OPP, off, n)
            f_copy(h, i).start()

    def near(i):
        for h in range(2):
            off, n = piece(h, i)
            send_n[pl.ds(off, n), :] = part_sum(RIGHT if h == 0 else LEFT, off, n)
            n_copy(h, i).start()

    def relay(i):
        for h in range(2):
            off, n = piece(h, i)
            mine = part_sum(LEFT if h == 0 else RIGHT, off, n)
            f_copy(h, i).wait_recv()
            recv_f[pl.ds(off, n), :] = recv_f[pl.ds(off, n), :] + mine
            r_copy(h, i).start()

    def account(z):
        zr = z.reshape(z.shape[0] // 8, 8, rows)
        old = m_acc[...]
        new = jnp.maximum(old, jnp.max(zr, axis=0))
        m_acc[...] = new
        s_acc[...] = s_acc[...] * jnp.exp(old - new) + jnp.sum(jnp.exp(zr - new[None]), axis=0)

    def settle_raw():
        for h in range(2):
            off, n = piece(h, 0)
            raw = raw_l if h == 0 else raw_r
            mine = part_sum(OWN, off, n)
            total_recv(raw, raw_recv.at[h])
            for other in range(2):
                mine = mine + jnp.dot(raw[other].astype(BF16), xnb[h, other], preferred_element_type=F32)
            r_copy(h, 0).wait_recv()
            z = mine + (recv_r if h == 0 else recv_l)[off:off + n, :]
            account(z)
            logits_ref[off:off + n, :] = z

    def settle(i):
        mine = [part_sum(OWN, *piece(h, i)) for h in range(2)]
        for h in range(2):
            off, n = piece(h, i)
            r_copy(h, i).wait_recv()
            n_copy(h, i).wait_recv()
            z = mine[h] + recv_l[pl.ds(off, n), :] + recv_r[pl.ds(off, n), :]
            account(z)
            logits_ref[pl.ds(off, n), :] = z

    for copy in small_in[3:]:
        copy.wait()
    tok = jnp.broadcast_to(tok_ref[...], (128, rows)).T

    def gather(step):
        for other in range(2):
            blk_chip = lax.rem(chip + jnp.where(step == 0, STEP_OF_SLOT[0], jnp.where(
                step == 1, STEP_OF_SLOT[1], jnp.where(step == 2, STEP_OF_SLOT[2], STEP_OF_SLOT[3]))), n_chip)
            blk = blk_chip * 2 + (1 - core if other else core)
            base = vp * (n_tp * n_block) + blk * n_block
            ref = e_oth if other else e_own
            acc = pick[...]
            for off in range(0, n_block, 512):
                n = min(512, n_block - off)
                for o, k in ((off, n // 128 * 128), (off + n // 128 * 128, n % 128)):
                    if k == 0:
                        continue
                    lane = lax.broadcasted_iota(jnp.int32, (rows, k), 1) + (base + o)
                    if k % 128 == 0:
                        want = jnp.concatenate([tok] * (k // 128), axis=1) if k > 128 else tok
                    else:
                        want = tok[:, :k]
                    hot = jnp.where(want == lane, 1.0, 0.0).astype(BF16)
                    acc = acc + jnp.dot(hot, ref[step, o:o + k, :], preferred_element_type=F32)
            pick[...] = acc

    def v_copy(src, dst, stage, j):
        return pltpu.make_async_remote_copy(
            src_ref=src, dst_ref=dst, send_sem=v_send.at[stage], recv_sem=v_recv.at[stage],
            device_id={"vp": lax.rem(vp + j, n_vp)}, device_id_type=MESH)

    def vp_start(buf, stage):
        for j in range(1, n_vp):
            v_copy(buf.at[vp], buf.at[vp], stage, j).start()

    def vp_wait(buf, stage):
        total_recv(buf.at[pl.ds(0, n_vp - 1)], v_recv.at[stage])

    def vp_drain(buf, stage):
        total_send(buf.at[pl.ds(0, n_vp - 1)], v_send.at[stage])

    def slabs_forward():
        own = pl.ds(pl.multiple_of(vp * xslab, 8), xslab)
        for d in range(2):
            slab_copy(d).wait_recv()
            for j in range(1, n_vp):
                v_copy(nb.at[d, own, :], nb.at[d, own, :], 3, j).start()

    nb_copy = pltpu.make_async_remote_copy(
        src_ref=nb, dst_ref=nb_par, send_sem=nb_send.at[0], recv_sem=nb_recv.at[0], device_id=partner, device_id_type=MESH)
    nb_rest = nb.at[:, pl.ds(0, width - xslab), :]

    def slabs_swap():
        total_recv(nb_rest, v_recv.at[3])
        nb_copy.start()
        for d in range(2):
            xnb[d, 0] = nb[d].astype(BF16)

    def slabs_done():
        nb_copy.wait_recv()
        for d in range(2):
            xnb[d, 1] = nb_par[d].astype(BF16)

    def rows_scatter():
        for j in range(1, n_vp):
            peer = lax.rem(vp + j, n_vp)
            v_copy(pick.at[pl.ds(pl.multiple_of(peer * slab, 8), slab), :], rs_buf.at[vp], 0, j).start()
        rs_buf[vp] = pick[pl.ds(pl.multiple_of(vp * slab, 8), slab), :]

    def rows_stats():
        vp_wait(rs_buf, 0)
        tot = rs_buf[0]
        for j in range(1, n_vp):
            tot = tot + rs_buf[j]
        ag_buf[vp] = tot
        lane = lax.broadcasted_iota(jnp.int32, (slab, 128), 1)
        both = jnp.where(lane == 0, jnp.sum(tot, axis=1, keepdims=True), jnp.sum(tot * tot, axis=1, keepdims=True)).T
        row_st[tp] = jnp.zeros((1, 256), F32)
        row_st[tp, :, 0:slab] = both[0:1]
        row_st[tp, :, 128:128 + slab] = both[1:2]
        tp_start(row_st, 1)

    def rows_norm():
        tp_wait(row_st, 1)
        tot = row_st[0]
        for j in range(1, n_tp):
            tot = tot + row_st[j]
        mu = tot[:, 0:128] / full_width
        rs = lax.rsqrt(tot[:, 128:256] / full_width - mu * mu + NORM_EPS)
        mu = jnp.broadcast_to(mu, (128, 128)).T[0:slab, 0:1]
        rs = jnp.broadcast_to(rs, (128, 128)).T[0:slab, 0:1]
        out = ((ag_buf[vp] - mu) * rs * eg_ref[...] + eb_ref[...]).astype(BF16)
        ag_buf[vp] = out.astype(F32)
        vp_start(ag_buf, 1)

    def rows_out():
        vp_wait(ag_buf, 1)
        for j in range(n_vp):
            next_ref[j * slab:(j + 1) * slab, :] = ag_buf[j].astype(BF16)

    pick[...] = jnp.zeros_like(pick)
    m_acc[...] = jnp.full_like(m_acc, -jnp.inf)
    s_acc[...] = jnp.zeros_like(s_acc)

    for q in range(2):
        load(OPP, False, q).wait()
        ex_copy(OPP, q).wait_recv()
        far(q)
        pl.semaphore_wait(hop.at[q], 2)
        for peer in (z_near, y_near)[q]:
            pl.semaphore_signal(hop.at[q + 1], inc=1, device_id=peer, device_id_type=MESH)
    for slot in (LEFT, RIGHT):
        ex_copy(slot, 0).wait_recv()
    far(2)
    relay(0)
    pl.semaphore_wait(hop.at[2], 2)
    for slot in (LEFT, RIGHT, OWN):
        load(slot, False, 1).wait()
        ex_copy(slot, 1).wait_recv()
    load(OWN, False, 0).wait()
    ex_copy(OWN, 0).wait_recv()

    def at(i, when, *steps):
        @pl.when(i == when)
        def _():
            for step in steps:
                step()

    def round_body(i, carry):
        near(i)

        @pl.when(i + 2 < n_round)
        def _():
            far(i + 2)

        relay(i)
        at(i, 1, slabs_forward)

        @pl.when(i <= 2)
        def _():
            gather(2 * i - 2)
            gather(2 * i - 1)

        at(i, 2, slabs_swap)
        at(i, 3, rows_scatter, slabs_done)
        at(i, 4, rows_stats, settle_raw)
        at(i, 6, rows_norm)

        @pl.when(i >= 3)
        def _():
            settle(i - 2)

        return carry

    lax.fori_loop(1, n_round, round_body, 0)

    def last_body(i, carry):
        settle(i)
        return carry

    lax.fori_loop(n_round - 2, n_round, last_body, 0)

    def merge(buf, n):
        top = buf[0]
        for j in range(1, n):
            top = jnp.maximum(top, buf[j])
        tot = jnp.exp(buf[0] - top)
        for j in range(1, n):
            tot = tot + jnp.exp(buf[j] - top)
        return top + jnp.log(tot)

    m8 = m_acc[...]
    top = jnp.max(m8, axis=0, keepdims=True)
    st_all[vp] = top + jnp.log(jnp.sum(s_acc[...] * jnp.exp(m8 - top), axis=0, keepdims=True))
    vp_start(st_all, 2)
    rows_out()
    hx_copy.wait_send()
    nb_copy.wait_send()
    total_send(e_out, ex_send.at[0])
    total_send(raw_l, raw_send.at[0])
    total_send(raw_r, raw_send.at[1])
    total_send(nb.at[0, pl.ds(0, 2 * xslab), :], sx_send.at[0])
    total_send(send_f, f_send.at[0])
    total_send(recv_f, r_send.at[0])
    total_send(send_n.at[pl.ds(0, tail0), :], n_send.at[0])
    tp_drain(st_ln, 0)
    tp_drain(row_st, 1)
    vp_drain(rs_buf, 0)
    vp_drain(ag_buf, 1)
    total_send(nb_rest, v_send.at[3])
    vp_wait(st_all, 2)
    st_lse[tp] = merge(st_all, n_vp)
    tp_start(st_lse, 2)
    vp_drain(st_all, 2)
    tp_wait(st_lse, 2)
    lse_ref[...] = merge(st_lse, n_tp)
    tp_drain(st_lse, 2)


def finish_kernel(n_piece, z_ref, lse_ref, next_ref, out_ref, sum_ref, row_ref, buf, sems):
    lse = lse_ref[...]
    n = z_ref.shape[0] // n_piece

    def put(j):
        part = pl.ds(j * n, n)
        return pltpu.make_async_copy(buf.at[part, :], out_ref.at[part, :], sems.at[j])

    small = [pltpu.make_async_copy(lse_ref, sum_ref, sems.at[n_piece]),
             pltpu.make_async_copy(next_ref, row_ref, sems.at[n_piece + 1])]
    for copy in small:
        copy.start()
    for j in range(n_piece):
        buf[j * n:(j + 1) * n, :] = z_ref[j * n:(j + 1) * n, :] - lse
        put(j).start()
    for copy in small:
        copy.wait()
    for j in range(n_piece):
        put(j).wait()


def solution(mesh):
    n_vp, n_tp = mesh.shape["vp"], mesh.shape["tp"]

    def per_device(hidden, lnf_gain, lnf_bias, emb_table, next_tok, eln_gain, eln_bias):
        rows, width = hidden.shape
        n_block = emb_table.shape[0] // n_tp
        slab = rows // n_vp
        n_round = n_block // 2 // CHUNK + 1
        small = n_block - 2 * (n_round - 1) * CHUNK
        dma = pltpu.SemaphoreType.DMA
        vmem = pl.BlockSpec(memory_space=pltpu.VMEM)
        logits, lse, next_in = pl.pallas_call(
            functools.partial(head_kernel, n_vp, n_tp, n_block, width * n_tp),
            out_shape=(
                pltpu.VMEM((n_block, rows), F32),
                pltpu.VMEM((1, rows), F32),
                pltpu.VMEM((rows, width), BF16),
            ),
            in_specs=[pl.BlockSpec(memory_space=pl.ANY)] * 7,
            out_specs=(vmem, vmem, vmem),
            scratch_shapes=[
                pltpu.VMEM((4, n_block, width), BF16),
                pltpu.VMEM((4, n_block, width), BF16),
                pltpu.VMEM((4, n_block, width), F32),
                pltpu.VMEM((4, n_block, width), F32),
                pltpu.VMEM((n_block, rows), F32),
                pltpu.VMEM((n_block, rows), F32),
                pltpu.VMEM((n_block, rows), F32),
                pltpu.VMEM((n_block, rows), F32),
                pltpu.VMEM((n_block, rows), F32),
                pltpu.VMEM((2, width, rows + 256), F32),
                pltpu.VMEM((2, width, rows), BF16),
                pltpu.VMEM((8, rows), F32),
                pltpu.VMEM((8, rows), F32),
                pltpu.VMEM((rows, width), F32),
                pltpu.VMEM((n_tp, 1, 2 * rows), F32),
                pltpu.VMEM((n_tp, 1, rows), F32),
                pltpu.VMEM((n_vp, 1, rows), F32),
                pltpu.VMEM((n_vp, slab, width), F32),
                pltpu.VMEM((n_tp, 1, 256), F32),
                pltpu.VMEM((n_vp, slab, width), F32),
                pltpu.VMEM((small, width), F32),
                pltpu.VMEM((2, small - small // 16 * 8, width), F32),
                pltpu.VMEM((2, small // 16 * 8, width), F32),
                pltpu.VMEM((width // n_vp, rows), F32),
                pltpu.VMEM((2, width, rows), F32),
                pltpu.VMEM((2, width, rows), F32),
                pltpu.VMEM((2, 2, width, rows), BF16),
                dma((2, 4, 2)), dma((1,)), dma((4, 2)), dma((1,)), dma((1,)),
                dma((1,)), dma((2, n_round)), dma((1,)), dma((1,)), dma((2, n_round)), dma((2, n_round)),
                dma((3,)), dma((3,)), dma((4,)), dma((4,)), dma((2,)), dma((2,)), dma((1,)), dma((2,)), dma((1,)), dma((1,)),
                pltpu.SemaphoreType.REGULAR((3,)),
                pltpu.VMEM((rows, width), BF16),
                pltpu.VMEM((1, width), F32),
                pltpu.VMEM((1, width), F32),
                pltpu.VMEM((1, rows), jnp.int32),
                pltpu.VMEM((1, width), F32),
                pltpu.VMEM((1, width), F32),
                dma((6,)),
            ],
            compiler_params=pltpu.CompilerParams(
                collective_id=0, has_side_effects=True, vmem_limit_bytes=57 * 1024 * 1024),
            cost_estimate=pl.CostEstimate(
                flops=4 * rows * n_block * n_tp * width, bytes_accessed=16 * n_block * n_tp * width, transcendentals=rows * n_block),
        )(hidden, lnf_gain[None, :], lnf_bias[None, :], emb_table, next_tok[None, :], eln_gain[None, :], eln_bias[None, :])
        n_piece = 5
        logprobs_t, log_sum, next_bf = pl.pallas_call(
            functools.partial(finish_kernel, n_piece),
            out_shape=(
                jax.ShapeDtypeStruct((n_block, rows), F32),
                jax.ShapeDtypeStruct((1, rows), F32),
                jax.ShapeDtypeStruct((rows, width), BF16),
            ),
            in_specs=[vmem, vmem, vmem],
            out_specs=(pl.BlockSpec(memory_space=pl.ANY),) * 3,
            scratch_shapes=[pltpu.VMEM((n_block, rows), F32), dma((n_piece + 2,))],
            compiler_params=pltpu.CompilerParams(vmem_limit_bytes=16 * 1024 * 1024),
        )(logits, lse, next_in)
        return logprobs_t.T, log_sum[0], next_bf

    return jax.shard_map(
        per_device,
        mesh=mesh,
        in_specs=(P("dp", "tp"), P("tp"), P("tp"), P("vp", "tp"), P("dp"), P("tp"), P("tp")),
        out_specs=(P("dp", ("vp", "tp")), P("dp"), P("dp", "tp")),
        check_vma=False,
    )
```

time: 158 us -> 154 us (0.975)
  Pallas kernels: 158 us -> 153 us
    pallas_call x1, Pallas kernels: 155 us -> 151 us  [per_device(): pl.pallas_call(functools.partial(head_kernel, n_vp, n_tp, n_block, width...]
where the time goes in v4:
time: 154 us
  Pallas kernels  153 us (99%)
    pallas_call x1, Pallas kernels, per_device(): pl.pallas_call(functools.partial(head_kernel, n_vp, n_tp, n_block, width...  151 us

profile of v4, /device:TPU:1, one launch (start us, length us, event | category | flops | bytes accessed | tf_op | source)
XLA Modules:
  0.0 153.7 jit_solution(5838994245342853164)
XLA Ops:
  0.6 151.0 %shard_map.94 = (f32[1960,512]{1,0:T(8,128)S(1)}, f32[1,512]{1,0:T(1,128)S(1)}, bf16[512,256]{1,0:T(8,128)(2,1)S(1)}) custom-call(bf16[512,256]{1,0:T(8,128)(2,1)} %hid_hbm.1, f32[1,256]{1,0:T(1,128)} %bitcast.10, f32[1,256]{1,0:T(1,128)} %bitcast.11, bf16[15680,256]{1,0:T(8,128)(2,1)} %emb_ref.1, s32[1,512]{1,0:T(1,128)} %bitcast.8, f32[1,256]{1,0:T(1,128)} %bitcast.12, ...), custom_call_target="tpu_custom_call" | custom-call | flops 8220835840 | bytes 64225280 | tf_op jit(solution)/shard_map/pallas_call | solution.py:501
  151.6 2.1 %shard_map.95 = (f32[1960,512]{1,0:T(8,128)}, f32[1,512]{1,0:T(1,128)}, bf16[512,256]{1,0:T(8,128)(2,1)}) custom-call(f32[1960,512]{1,0:T(8,128)S(1)} %get-tuple-element.9.z_ref, f32[1,512]{1,0:T(1,128)S(1)} %get-tuple-element.10.lse_ref, bf16[512,256]{1,0:T(8,128)(2,1)S(1)} %get-tuple-element.11.next_ref), custom_call_target="tpu_custom_call" | custom-call | tf_op jit(solution)/shard_map/pallas_call | solution.py:556

commit v5 on v4

--- a/solution.py
+++ b/solution.py
@@ -25,9 +25,9 @@
                 hx, xn, m_acc, s_acc, pick, st_ln, st_lse, st_all, rs_buf, row_st, ag_buf,
                 raw_src, raw_l, raw_r, slab_src, nb, nb_par, xnb,
                 ld_sem, ex_send, ex_recv, hx_send, hx_recv,
-                f_send, f_recv, n_send, r_send, l_recv, r_recv,
+                f_send, f_recv, n_send, r_send, in_recv,
                 t_send, t_recv, v_send, v_recv, raw_send, raw_recv, sx_send, sx_recv, nb_send, nb_recv, hop,
-                hid_ref, g_ref, b_ref, tok_ref, eg_ref, eb_ref, in_sem):
+                hid_ref, tok_ref, vec_ref, in_sem):
     vp = lax.axis_index("vp")
     tp = lax.axis_index("tp")
     core = lax.rem(tp, 2)
@@ -65,27 +65,26 @@
     for peer in y_near + z_near:
         pl.semaphore_signal(barrier, inc=1, device_id=peer, device_id_type=MESH)
 
-    parts = ((tail0, small), (0, tail0))
-
-    def load(slot, other, q):
+    parts = ((tail0, small), (0, tail0), (0, n_block))
+
+    def load(slot, other, q, sem):
         blk = lax.rem(chip + STEP_OF_SLOT[slot], n_chip) * 2 + (1 - core if other else core)
         off, n = parts[q]
         src = emb_ref.at[pl.ds(pl.multiple_of(blk * n_block + off, 8), n), :]
         dst = (e_oth if other else e_own).at[slot, pl.ds(off, n), :]
-        return pltpu.make_async_copy(src, dst, ld_sem.at[int(other), slot, q])
-
-    small_in = [pltpu.make_async_copy(src, dst, in_sem.at[k]) for k, (src, dst) in enumerate((
-        (hid_hbm, hid_ref), (g_hbm, g_ref), (b_hbm, b_ref), (tok_hbm, tok_ref), (eg_hbm, eg_ref), (eb_hbm, eb_ref)))]
-    for copy in small_in[:3]:
-        copy.start()
+        return pltpu.make_async_copy(src, dst, ld_sem.at[sem])
+
+    hid_copy = pltpu.make_async_copy(hid_hbm, hid_ref, in_sem.at[0])
+    tok_copy = pltpu.make_async_copy(tok_hbm, tok_ref, in_sem.at[1])
+    hid_copy.start()
+    for k, src in enumerate((g_hbm, b_hbm, eg_hbm, eb_hbm)):
+        pltpu.make_async_copy(src, vec_ref.at[k], in_sem.at[2]).start()
     for slot in (RIGHT, LEFT):
-        load(slot, True, 0).start()
-        load(slot, False, 0).start()
-    for slot, q in ((OPP, 0), (OPP, 1), (LEFT, 1), (RIGHT, 1), (OWN, 0), (OWN, 1)):
-        load(slot, True, q).start()
-        load(slot, False, q).start()
-    for copy in small_in[3:]:
-        copy.start()
+        load(slot, True, 0, 0).start()
+        load(slot, False, 0, 0).start()
+
+    def total_load(ref, sem):
+        pltpu.make_async_copy(ref, ref, sem).wait()
 
     def total_recv(ref, sem):
         pltpu.make_async_remote_copy(src_ref=ref, dst_ref=ref, send_sem=sem, recv_sem=sem,
@@ -95,12 +94,9 @@
         pltpu.make_async_remote_copy(src_ref=ref, dst_ref=ref, send_sem=sem, recv_sem=sem,
                                      device_id=partner, device_id_type=MESH).wait_send()
 
-    for copy in small_in[:3]:
-        copy.wait()
+    hid_copy.wait()
     h_t = hid_ref[...].astype(F32).T
     hx[0, :, 0:rows] = h_t
-    hx[0, :, rows:rows + 128] = jnp.broadcast_to(g_ref[...], (128, width)).T
-    hx[0, :, rows + 128:rows + 256] = jnp.broadcast_to(b_ref[...], (128, width)).T
     st_ln[tp, :, 0:rows] = jnp.sum(h_t, axis=0, keepdims=True)
     st_ln[tp, :, rows:2 * rows] = jnp.sum(h_t * h_t, axis=0, keepdims=True)
 
@@ -108,9 +104,15 @@
         off, n = parts[q]
         e_out[slot, off:off + n, :] = e_oth[slot, off:off + n, :].astype(F32)
 
+    total_load(e_own.at[0, pl.ds(0, 4 * small), :], ld_sem.at[0])
+    for slot, q, sem in ((OPP, 2, 1), (LEFT, 1, 3), (RIGHT, 1, 3), (OWN, 2, 4)):
+        load(slot, True, q, sem).start()
+        if slot == OPP:
+            load(slot, False, q, 2).start()
+    for slot, q, sem in ((LEFT, 1, 5), (RIGHT, 1, 5), (OWN, 2, 6)):
+        load(slot, False, q, sem).start()
+    tok_copy.start()
     for slot in (RIGHT, LEFT):
-        load(slot, True, 0).wait()
-        load(slot, False, 0).wait()
         convert(slot, 0)
         off, n = piece(0 if slot == RIGHT else 1, 0)
         raw_src[off - tail0:off - tail0 + n, :] = e_own[slot, off:off + n, :].astype(F32)
@@ -121,7 +123,7 @@
         to = (right_chip if slot == RIGHT else left_chip) * 2 + (1 - core if other else core)
         return pltpu.make_async_remote_copy(
             src_ref=src, dst_ref=(raw_l if slot == RIGHT else raw_r).at[int(other)],
-            send_sem=raw_send.at[int(slot == LEFT)], recv_sem=raw_recv.at[int(slot == LEFT)],
+            send_sem=raw_send.at[0], recv_sem=raw_recv.at[int(slot == LEFT)],
             device_id={"tp": to}, device_id_type=MESH)
 
     pl.semaphore_wait(barrier, n_tp + 3)
@@ -143,6 +145,9 @@
         for slot in (RIGHT, LEFT):
             raw_copy(slot, other).start()
 
+    total_load(vec_ref, in_sem.at[2])
+    hx[0, :, rows:rows + 128] = jnp.broadcast_to(vec_ref[0], (128, width)).T
+    hx[0, :, rows + 128:rows + 256] = jnp.broadcast_to(vec_ref[1], (128, width)).T
     hx_copy = pltpu.make_async_remote_copy(
         src_ref=hx.at[0], dst_ref=hx.at[1], send_sem=hx_send.at[0], recv_sem=hx_recv.at[0],
         device_id=partner, device_id_type=MESH)
@@ -150,17 +155,26 @@
     for peer in y_near:
         pl.semaphore_signal(hop.at[0], inc=1, device_id=peer, device_id_type=MESH)
 
-    def ex_copy(slot, q):
+    def ex_copy(slot, q, sem):
         off, n = parts[q]
         return pltpu.make_async_remote_copy(
             src_ref=e_out.at[slot, pl.ds(off, n), :], dst_ref=e_in.at[slot, pl.ds(off, n), :],
-            send_sem=ex_send.at[0], recv_sem=ex_recv.at[slot, q], device_id=partner, device_id_type=MESH)
-
-    for slot, q in ((OPP, 0), (OPP, 1), (LEFT, 0), (RIGHT, 0), (LEFT, 1), (RIGHT, 1), (OWN, 0), (OWN, 1)):
-        if q == 1 or slot in (OPP, OWN):
-            load(slot, True, q).wait()
-            convert(slot, q)
-        ex_copy(slot, q).start()
+            send_sem=ex_send.at[0], recv_sem=ex_recv.at[sem], device_id=partner, device_id_type=MESH)
+
+    load(OPP, True, 2, 1).wait()
+    for q in range(2):
+        convert(OPP, q)
+        ex_copy(OPP, q, q).start()
+    for slot in (LEFT, RIGHT):
+        ex_copy(slot, 0, 2).start()
+    sides = e_oth.at[pl.ds(LEFT, 2), pl.ds(0, tail0), :]
+    total_load(sides, ld_sem.at[3])
+    for slot in (LEFT, RIGHT):
+        convert(slot, 1)
+        ex_copy(slot, 1, 3).start()
+    load(OWN, True, 2, 4).wait()
+    convert(OWN, 2)
+    ex_copy(OWN, 2, 4).start()
 
     tp_wait(st_ln, 0)
     total = st_ln[0]
@@ -198,7 +212,7 @@
         off, n = piece(h, i)
         return pltpu.make_async_remote_copy(
             src_ref=send_f.at[pl.ds(off, n), :], dst_ref=recv_f.at[pl.ds(off, n), :],
-            send_sem=f_send.at[0], recv_sem=f_recv.at[h, i],
+            send_sem=f_send.at[0], recv_sem=f_recv.at[i],
             device_id=left if h == 0 else right, device_id_type=MESH)
 
     def r_copy(h, i):
@@ -206,7 +220,7 @@
         dst = (recv_r if h == 0 else recv_l).at[pl.ds(off, n), :]
         return pltpu.make_async_remote_copy(
             src_ref=recv_f.at[pl.ds(off, n), :], dst_ref=dst,
-            send_sem=r_send.at[0], recv_sem=(r_recv if h == 0 else l_recv).at[h, i],
+            send_sem=r_send.at[0], recv_sem=in_recv.at[i],
             device_id=left if h == 0 else right, device_id_type=MESH)
 
     def n_copy(h, i):
@@ -214,7 +228,7 @@
         dst = (recv_l if h == 0 else recv_r).at[pl.ds(off, n), :]
         return pltpu.make_async_remote_copy(
             src_ref=send_n.at[pl.ds(off, n), :], dst_ref=dst,
-            send_sem=n_send.at[0], recv_sem=(l_recv if h == 0 else r_recv).at[h, i],
+            send_sem=n_send.at[0], recv_sem=in_recv.at[i],
             device_id=right if h == 0 else left, device_id_type=MESH)
 
     def far(i):
@@ -230,11 +244,11 @@
             n_copy(h, i).start()
 
     def relay(i):
+        mine = [part_sum(LEFT if h == 0 else RIGHT, *piece(h, i)) for h in range(2)]
+        total_recv(recv_f.at[pl.ds(0, small if isinstance(i, int) else 2 * CHUNK), :], f_recv.at[i])
         for h in range(2):
             off, n = piece(h, i)
-            mine = part_sum(LEFT if h == 0 else RIGHT, off, n)
-            f_copy(h, i).wait_recv()
-            recv_f[pl.ds(off, n), :] = recv_f[pl.ds(off, n), :] + mine
+            recv_f[pl.ds(off, n), :] = recv_f[pl.ds(off, n), :] + mine[h]
             r_copy(h, i).start()
 
     def account(z):
@@ -248,27 +262,26 @@
         for h in range(2):
             off, n = piece(h, 0)
             raw = raw_l if h == 0 else raw_r
+            if h == 0:
+                total_recv(recv_l.at[pl.ds(0, small), :], in_recv.at[0])
             mine = part_sum(OWN, off, n)
             total_recv(raw, raw_recv.at[h])
             for other in range(2):
                 mine = mine + jnp.dot(raw[other].astype(BF16), xnb[h, other], preferred_element_type=F32)
-            r_copy(h, 0).wait_recv()
             z = mine + (recv_r if h == 0 else recv_l)[off:off + n, :]
             account(z)
             logits_ref[off:off + n, :] = z
 
     def settle(i):
         mine = [part_sum(OWN, *piece(h, i)) for h in range(2)]
+        total_recv(recv_l.at[pl.ds(0, 4 * CHUNK), :], in_recv.at[i])
         for h in range(2):
             off, n = piece(h, i)
-            r_copy(h, i).wait_recv()
-            n_copy(h, i).wait_recv()
             z = mine[h] + recv_l[pl.ds(off, n), :] + recv_r[pl.ds(off, n), :]
             account(z)
             logits_ref[pl.ds(off, n), :] = z
 
-    for copy in small_in[3:]:
-        copy.wait()
+    tok_copy.wait()
     tok = jnp.broadcast_to(tok_ref[...], (128, rows)).T
 
     def gather(step):
@@ -358,7 +371,7 @@
         rs = lax.rsqrt(tot[:, 128:256] / full_width - mu * mu + NORM_EPS)
         mu = jnp.broadcast_to(mu, (128, 128)).T[0:slab, 0:1]
         rs = jnp.broadcast_to(rs, (128, 128)).T[0:slab, 0:1]
-        out = ((ag_buf[vp] - mu) * rs * eg_ref[...] + eb_ref[...]).astype(BF16)
+        out = ((ag_buf[vp] - mu) * rs * vec_ref[2] + vec_ref[3]).astype(BF16)
         ag_buf[vp] = out.astype(F32)
         vp_start(ag_buf, 1)
 
@@ -371,23 +384,21 @@
     m_acc[...] = jnp.full_like(m_acc, -jnp.inf)
     s_acc[...] = jnp.zeros_like(s_acc)
 
+    load(OPP, False, 2, 2).wait()
     for q in range(2):
-        load(OPP, False, q).wait()
-        ex_copy(OPP, q).wait_recv()
+        ex_copy(OPP, q, q).wait_recv()
         far(q)
         pl.semaphore_wait(hop.at[q], 2)
         for peer in (z_near, y_near)[q]:
             pl.semaphore_signal(hop.at[q + 1], inc=1, device_id=peer, device_id_type=MESH)
-    for slot in (LEFT, RIGHT):
-        ex_copy(slot, 0).wait_recv()
+    total_recv(e_in.at[pl.ds(LEFT, 2), pl.ds(tail0, small), :], ex_recv.at[2])
     far(2)
     relay(0)
     pl.semaphore_wait(hop.at[2], 2)
-    for slot in (LEFT, RIGHT, OWN):
-        load(slot, False, 1).wait()
-        ex_copy(slot, 1).wait_recv()
-    load(OWN, False, 0).wait()
-    ex_copy(OWN, 0).wait_recv()
+    total_load(sides, ld_sem.at[5])
+    total_recv(e_in.at[pl.ds(LEFT, 2), pl.ds(0, tail0), :], ex_recv.at[3])
+    load(OWN, False, 2, 6).wait()
+    ex_copy(OWN, 2, 4).wait_recv()
 
     def at(i, when, *steps):
         @pl.when(i == when)
@@ -446,8 +457,7 @@
     hx_copy.wait_send()
     nb_copy.wait_send()
     total_send(e_out, ex_send.at[0])
-    total_send(raw_l, raw_send.at[0])
-    total_send(raw_r, raw_send.at[1])
+    total_send(e_in.at[0, pl.ds(0, 2 * small), :], raw_send.at[0])
     total_send(nb.at[0, pl.ds(0, 2 * xslab), :], sx_send.at[0])
     total_send(send_f, f_send.at[0])
     total_send(recv_f, r_send.at[0])
@@ -535,17 +545,14 @@
                 pltpu.VMEM((2, width, rows), F32),
                 pltpu.VMEM((2, width, rows), F32),
                 pltpu.VMEM((2, 2, width, rows), BF16),
-                dma((2, 4, 2)), dma((1,)), dma((4, 2)), dma((1,)), dma((1,)),
-                dma((1,)), dma((2, n_round)), dma((1,)), dma((1,)), dma((2, n_round)), dma((2, n_round)),
-                dma((3,)), dma((3,)), dma((4,)), dma((4,)), dma((2,)), dma((2,)), dma((1,)), dma((2,)), dma((1,)), dma((1,)),
+                dma((7,)), dma((1,)), dma((5,)), dma((1,)), dma((1,)),
+                dma((1,)), dma((n_round,)), dma((1,)), dma((1,)), dma((n_round,)),
+                dma((3,)), dma((3,)), dma((4,)), dma((4,)), dma((1,)), dma((2,)), dma((1,)), dma((2,)), dma((1,)), dma((1,)),
                 pltpu.SemaphoreType.REGULAR((3,)),
                 pltpu.VMEM((rows, width), BF16),
-                pltpu.VMEM((1, width), F32),
-                pltpu.VMEM((1, width), F32),
                 pltpu.VMEM((1, rows), jnp.int32),
-                pltpu.VMEM((1, width), F32),
-                pltpu.VMEM((1, width), F32),
-                dma((6,)),
+                pltpu.VMEM((4, 1, width), F32),
+                dma((3,)),
             ],
             compiler_params=pltpu.CompilerParams(
                 collective_id=0, has_side_effects=True, vmem_limit_bytes=57 * 1024 * 1024),

time: 154 us -> 152 us (0.987)
    pallas_call x1, Pallas kernels: 151 us -> 149 us  [per_device(): pl.pallas_call(functools.partial(head_kernel, n_vp, n_tp, n_block, width...]
where the time goes in v5:
time: 152 us
  Pallas kernels  152 us (100%)
    pallas_call x1, Pallas kernels, per_device(): pl.pallas_call(functools.partial(head_kernel, n_vp, n_tp, n_block, width...  149 us

profile of v5, /device:TPU:1, one launch (start us, length us, event | category | flops | bytes accessed | tf_op | source)
XLA Modules:
  0.0 152.2 jit_solution(1139320168816540863)
XLA Ops:
  0.6 149.4 %shard_map.94 = (f32[1960,512]{1,0:T(8,128)S(1)}, f32[1,512]{1,0:T(1,128)S(1)}, bf16[512,256]{1,0:T(8,128)(2,1)S(1)}) custom-call(bf16[512,256]{1,0:T(8,128)(2,1)} %hid_hbm.1, f32[1,256]{1,0:T(1,128)} %bitcast.10, f32[1,256]{1,0:T(1,128)} %bitcast.11, bf16[15680,256]{1,0:T(8,128)(2,1)} %emb_ref.1, s32[1,512]{1,0:T(1,128)} %bitcast.8, f32[1,256]{1,0:T(1,128)} %bitcast.12, ...), custom_call_target="tpu_custom_call" | custom-call | flops 8220835840 | bytes 64225280 | tf_op jit(solution)/shard_map/pallas_call | solution.py:511
  150.1 2.1 %shard_map.95 = (f32[1960,512]{1,0:T(8,128)}, f32[1,512]{1,0:T(1,128)}, bf16[512,256]{1,0:T(8,128)(2,1)}) custom-call(f32[1960,512]{1,0:T(8,128)S(1)} %get-tuple-element.9.z_ref, f32[1,512]{1,0:T(1,128)S(1)} %get-tuple-element.10.lse_ref, bf16[512,256]{1,0:T(8,128)(2,1)S(1)} %get-tuple-element.11.next_ref), custom_call_target="tpu_custom_call" | custom-call | tf_op jit(solution)/shard_map/pallas_call | solution.py:563

commit v6 on v5

--- a/solution.py
+++ b/solution.py
@@ -49,13 +49,13 @@
     half = (n_block // 2) // CHUNK
     n_round = half + 1
     small = n_block - 2 * half * CHUNK
-    small2 = (small // 16) * 8
-    small1 = small - small2
+    small1 = (small // 16) * 8
+    small2 = small - small1
     tail0 = 2 * half * CHUNK
 
     def piece(h, i):
         if isinstance(i, int) and i == 0:
-            return (tail0 + small2, small1) if h == 0 else (tail0, small2)
+            return (tail0, small1) if h == 0 else (tail0 + small1, small2)
         off = h * half * CHUNK + (i - 1) * CHUNK
         return (off if isinstance(i, int) else pl.multiple_of(off, CHUNK)), CHUNK
 
@@ -451,8 +451,21 @@
 
     m8 = m_acc[...]
     top = jnp.max(m8, axis=0, keepdims=True)
-    st_all[vp] = top + jnp.log(jnp.sum(s_acc[...] * jnp.exp(m8 - top), axis=0, keepdims=True))
-    vp_start(st_all, 2)
+    mine = vp * 2 + core
+    st_all[mine] = top + jnp.log(jnp.sum(s_acc[...] * jnp.exp(m8 - top), axis=0, keepdims=True))
+
+    def collect(peer):
+        return pltpu.make_async_remote_copy(
+            src_ref=st_all.at[mine], dst_ref=st_all.at[mine], send_sem=v_send.at[2], recv_sem=v_recv.at[2],
+            device_id={"vp": peer, "tp": chip * 2 + 1}, device_id_type=MESH)
+
+    for j in range(1, n_vp):
+        collect(lax.rem(vp + j, n_vp)).start()
+
+    @pl.when(core == 0)
+    def _():
+        collect(vp).start()
+
     rows_out()
     hx_copy.wait_send()
     nb_copy.wait_send()
@@ -467,13 +480,25 @@
     vp_drain(rs_buf, 0)
     vp_drain(ag_buf, 1)
     total_send(nb_rest, v_send.at[3])
-    vp_wait(st_all, 2)
-    st_lse[tp] = merge(st_all, n_vp)
-    tp_start(st_lse, 2)
-    vp_drain(st_all, 2)
-    tp_wait(st_lse, 2)
-    lse_ref[...] = merge(st_lse, n_tp)
-    tp_drain(st_lse, 2)
+
+    @pl.when(core == 1)
+    def _():
+        total_recv(st_all.at[pl.ds(0, 2 * n_vp - 1)], v_recv.at[2])
+        st_lse[chip] = merge(st_all, 2 * n_vp)
+        for peer in [lax.rem(tp + j, n_tp) for j in range(1, n_tp)]:
+            pltpu.make_async_remote_copy(
+                src_ref=st_lse.at[chip], dst_ref=st_lse.at[chip], send_sem=t_send.at[2], recv_sem=t_recv.at[2],
+                device_id={"tp": peer}, device_id_type=MESH).start()
+        total_send(st_all.at[pl.ds(0, n_vp - 1)], v_send.at[2])
+        total_recv(st_lse.at[pl.ds(0, n_chip - 1)], t_recv.at[2])
+        total_send(st_all.at[pl.ds(0, n_tp - 1)], t_send.at[2])
+
+    @pl.when(core == 0)
+    def _():
+        total_send(st_all.at[pl.ds(0, n_vp)], v_send.at[2])
+        total_recv(st_lse, t_recv.at[2])
+
+    lse_ref[...] = merge(st_lse, n_chip)
 
 
 def finish_kernel(n_piece, z_ref, lse_ref, next_ref, out_ref, sum_ref, row_ref, buf, sems):
@@ -533,14 +558,14 @@
                 pltpu.VMEM((8, rows), F32),
                 pltpu.VMEM((rows, width), F32),
                 pltpu.VMEM((n_tp, 1, 2 * rows), F32),
-                pltpu.VMEM((n_tp, 1, rows), F32),
-                pltpu.VMEM((n_vp, 1, rows), F32),
+                pltpu.VMEM((n_tp // 2, 1, rows), F32),
+                pltpu.VMEM((2 * n_vp, 1, rows), F32),
                 pltpu.VMEM((n_vp, slab, width), F32),
                 pltpu.VMEM((n_tp, 1, 256), F32),
                 pltpu.VMEM((n_vp, slab, width), F32),
                 pltpu.VMEM((small, width), F32),
+                pltpu.VMEM((2, small // 16 * 8, width), F32),
                 pltpu.VMEM((2, small - small // 16 * 8, width), F32),
-                pltpu.VMEM((2, small // 16 * 8, width), F32),
                 pltpu.VMEM((width // n_vp, rows), F32),
                 pltpu.VMEM((2, width, rows), F32),
                 pltpu.VMEM((2, width, rows), F32),

time: 152 us -> 151 us (level)
  Pallas kernels: 152 us -> 150 us
where the time goes in v6:
time: 151 us
  Pallas kernels  150 us (99%)
    pallas_call x1, Pallas kernels, per_device(): pl.pallas_call(functools.partial(head_kernel, n_vp, n_tp, n_block, width...  148 us

profile of v6, /device:TPU:1, one launch (start us, length us, event | category | flops | bytes accessed | tf_op | source)
XLA Modules:
  0.0 151.0 jit_solution(2966313401907909390)
XLA Ops:
  0.6 148.2 %shard_map.94 = (f32[1960,512]{1,0:T(8,128)S(1)}, f32[1,512]{1,0:T(1,128)S(1)}, bf16[512,256]{1,0:T(8,128)(2,1)S(1)}) custom-call(bf16[512,256]{1,0:T(8,128)(2,1)} %hid_hbm.1, f32[1,256]{1,0:T(1,128)} %bitcast.10, f32[1,256]{1,0:T(1,128)} %bitcast.11, bf16[15680,256]{1,0:T(8,128)(2,1)} %emb_ref.1, s32[1,512]{1,0:T(1,128)} %bitcast.8, f32[1,256]{1,0:T(1,128)} %bitcast.12, ...), custom_call_target="tpu_custom_call" | custom-call | flops 8220835840 | bytes 64225280 | tf_op jit(solution)/shard_map/pallas_call | solution.py:536
  148.9 2.1 %shard_map.95 = (f32[1960,512]{1,0:T(8,128)}, f32[1,512]{1,0:T(1,128)}, bf16[512,256]{1,0:T(8,128)(2,1)}) custom-call(f32[1960,512]{1,0:T(8,128)S(1)} %get-tuple-element.9.z_ref, f32[1,512]{1,0:T(1,128)S(1)} %get-tuple-element.10.lse_ref, bf16[512,256]{1,0:T(8,128)(2,1)S(1)} %get-tuple-element.11.next_ref), custom_call_target="tpu_custom_call" | custom-call | tf_op jit(solution)/shard_map/pallas_call | solution.py:588

commit v7 on v6

--- a/solution.py
+++ b/solution.py
@@ -15,6 +15,7 @@
 
 OPP, LEFT, RIGHT, OWN = 0, 1, 2, 3
 SIDE = 4
+N_HOP = 5
 STEP_OF_SLOT = (2, 3, 1, 0)
 
 
@@ -35,7 +36,7 @@
     n_chip = n_tp // 2
     rows, width = hid_hbm.shape
     slab = rows // n_vp
-    xslab = width // n_vp
+    xslab = width // (n_vp // 2)
     left_chip = lax.rem(chip + n_chip - 1, n_chip)
     right_chip = lax.rem(chip + 1, n_chip)
     left = {"tp": left_chip * 2 + core}
@@ -44,8 +45,23 @@
     y = lax.rem(vp, SIDE)
     z = vp // SIDE
     n_z = n_vp // SIDE
-    y_near = [{"vp": z * SIDE + lax.rem(y + d, SIDE)} for d in (1, SIDE - 1)]
-    z_near = [{"vp": lax.rem(z + d, n_z) * SIDE + y} for d in (1, n_z - 1)]
+    near_by = ((y > 0, {"vp": lax.rem(vp + n_vp - 1, n_vp)}), (y < SIDE - 1, {"vp": lax.rem(vp + 1, n_vp)}),
+               (z > 0, {"vp": lax.rem(vp + n_vp - SIDE, n_vp)}), (z < n_z - 1, {"vp": lax.rem(vp + SIDE, n_vp)}))
+    n_near = sum(jnp.where(there, 1, 0) for there, _ in near_by)
+
+    def tell_near(sem):
+        for there, peer in near_by:
+            @pl.when(there)
+            def _(peer=peer):
+                pl.semaphore_signal(sem, inc=1, device_id=peer, device_id_type=MESH)
+
+    def hear_near(step):
+        pl.semaphore_wait(hop.at[step], n_near)
+        if step + 1 < N_HOP:
+            tell_near(hop.at[step + 1])
+
+    n_carry = n_vp // 2
+    carries = vp < n_carry
     half = (n_block // 2) // CHUNK
     n_round = half + 1
     small = n_block - 2 * half * CHUNK
@@ -62,8 +78,7 @@
     barrier = pltpu.get_barrier_semaphore()
     for j in range(1, n_tp):
         pl.semaphore_signal(barrier, inc=1, device_id={"tp": lax.rem(tp + j, n_tp)}, device_id_type=MESH)
-    for peer in y_near + z_near:
-        pl.semaphore_signal(barrier, inc=1, device_id=peer, device_id_type=MESH)
+    tell_near(barrier)
 
     parts = ((tail0, small), (0, tail0), (0, n_block))
 
@@ -126,7 +141,7 @@
             send_sem=raw_send.at[0], recv_sem=raw_recv.at[int(slot == LEFT)],
             device_id={"tp": to}, device_id_type=MESH)
 
-    pl.semaphore_wait(barrier, n_tp + 3)
+    pl.semaphore_wait(barrier, n_tp - 1 + n_near)
 
     def tp_start(buf, stage):
         for j in range(1, n_tp):
@@ -152,8 +167,7 @@
         src_ref=hx.at[0], dst_ref=hx.at[1], send_sem=hx_send.at[0], recv_sem=hx_recv.at[0],
         device_id=partner, device_id_type=MESH)
     hx_copy.start()
-    for peer in y_near:
-        pl.semaphore_signal(hop.at[0], inc=1, device_id=peer, device_id_type=MESH)
+    tell_near(hop.at[0])
 
     def ex_copy(slot, q, sem):
         off, n = parts[q]
@@ -196,9 +210,13 @@
             send_sem=sx_send.at[0], recv_sem=sx_recv.at[d], device_id=right if d == 0 else left, device_id_type=MESH)
 
     norm(0)
-    slab_src[...] = xn[0, pl.ds(pl.multiple_of(vp * xslab, 8), xslab), :].astype(F32)
-    for d in range(2):
-        slab_copy(d).start()
+
+    @pl.when(carries)
+    def _():
+        slab_src[...] = xn[0, pl.ds(pl.multiple_of(vp * xslab, 32), xslab), :].astype(F32)
+        for d in range(2):
+            slab_copy(d).start()
+
     hx_copy.wait_recv()
     norm(1)
 
@@ -322,18 +340,28 @@
         total_send(buf.at[pl.ds(0, n_vp - 1)], v_send.at[stage])
 
     def slabs_forward():
-        own = pl.ds(pl.multiple_of(vp * xslab, 8), xslab)
-        for d in range(2):
-            slab_copy(d).wait_recv()
-            for j in range(1, n_vp):
-                v_copy(nb.at[d, own, :], nb.at[d, own, :], 3, j).start()
+        hear_near(N_HOP - 1)
+
+        @pl.when(carries)
+        def _():
+            own = pl.ds(pl.multiple_of(vp * xslab, 8), xslab)
+            for d in range(2):
+                slab_copy(d).wait_recv()
+                for j in range(1, n_vp):
+                    v_copy(nb.at[d, own, :], nb.at[d, own, :], 3, j).start()
 
     nb_copy = pltpu.make_async_remote_copy(
         src_ref=nb, dst_ref=nb_par, send_sem=nb_send.at[0], recv_sem=nb_recv.at[0], device_id=partner, device_id_type=MESH)
-    nb_rest = nb.at[:, pl.ds(0, width - xslab), :]
 
     def slabs_swap():
-        total_recv(nb_rest, v_recv.at[3])
+        @pl.when(carries)
+        def _():
+            total_recv(nb.at[:, pl.ds(0, width - xslab), :], v_recv.at[3])
+
+        @pl.when(jnp.logical_not(carries))
+        def _():
+            total_recv(nb, v_recv.at[3])
+
         nb_copy.start()
         for d in range(2):
             xnb[d, 0] = nb[d].astype(BF16)
@@ -388,13 +416,12 @@
     for q in range(2):
         ex_copy(OPP, q, q).wait_recv()
         far(q)
-        pl.semaphore_wait(hop.at[q], 2)
-        for peer in (z_near, y_near)[q]:
-            pl.semaphore_signal(hop.at[q + 1], inc=1, device_id=peer, device_id_type=MESH)
+        hear_near(q)
     total_recv(e_in.at[pl.ds(LEFT, 2), pl.ds(tail0, small), :], ex_recv.at[2])
     far(2)
+    hear_near(2)
     relay(0)
-    pl.semaphore_wait(hop.at[2], 2)
+    hear_near(3)
     total_load(sides, ld_sem.at[5])
     total_recv(e_in.at[pl.ds(LEFT, 2), pl.ds(0, tail0), :], ex_recv.at[3])
     load(OWN, False, 2, 6).wait()
@@ -459,8 +486,10 @@
             src_ref=st_all.at[mine], dst_ref=st_all.at[mine], send_sem=v_send.at[2], recv_sem=v_recv.at[2],
             device_id={"vp": peer, "tp": chip * 2 + 1}, device_id_type=MESH)
 
-    for j in range(1, n_vp):
-        collect(lax.rem(vp + j, n_vp)).start()
+    shifts = sorted(((dz, dy) for dz in range(n_z) for dy in range(SIDE) if dz or dy),
+                    key=lambda d: -min(d[0], n_z - d[0]) - min(d[1], SIDE - d[1]))
+    for dz, dy in shifts:
+        collect(lax.rem(z + dz, n_z) * SIDE + lax.rem(y + dy, SIDE)).start()
 
     @pl.when(core == 0)
     def _():
@@ -471,7 +500,12 @@
     nb_copy.wait_send()
     total_send(e_out, ex_send.at[0])
     total_send(e_in.at[0, pl.ds(0, 2 * small), :], raw_send.at[0])
-    total_send(nb.at[0, pl.ds(0, 2 * xslab), :], sx_send.at[0])
+
+    @pl.when(carries)
+    def _():
+        total_send(nb.at[0, pl.ds(0, 2 * xslab), :], sx_send.at[0])
+        total_send(send_f.at[pl.ds(0, 2 * (n_vp - 1) * xslab), :], v_send.at[3])
+
     total_send(send_f, f_send.at[0])
     total_send(recv_f, r_send.at[0])
     total_send(send_n.at[pl.ds(0, tail0), :], n_send.at[0])
@@ -479,13 +513,12 @@
     tp_drain(row_st, 1)
     vp_drain(rs_buf, 0)
     vp_drain(ag_buf, 1)
-    total_send(nb_rest, v_send.at[3])
 
     @pl.when(core == 1)
     def _():
         total_recv(st_all.at[pl.ds(0, 2 * n_vp - 1)], v_recv.at[2])
         st_lse[chip] = merge(st_all, 2 * n_vp)
-        for peer in [lax.rem(tp + j, n_tp) for j in range(1, n_tp)]:
+        for peer in [lax.rem(tp + j, n_tp) for j in (3, 4, 1, 2, 5, 6, 7)]:
             pltpu.make_async_remote_copy(
                 src_ref=st_lse.at[chip], dst_ref=st_lse.at[chip], send_sem=t_send.at[2], recv_sem=t_recv.at[2],
                 device_id={"tp": peer}, device_id_type=MESH).start()
@@ -566,14 +599,14 @@
                 pltpu.VMEM((small, width), F32),
                 pltpu.VMEM((2, small // 16 * 8, width), F32),
                 pltpu.VMEM((2, small - small // 16 * 8, width), F32),
-                pltpu.VMEM((width // n_vp, rows), F32),
+                pltpu.VMEM((width // (n_vp // 2), rows), F32),
                 pltpu.VMEM((2, width, rows), F32),
                 pltpu.VMEM((2, width, rows), F32),
                 pltpu.VMEM((2, 2, width, rows), BF16),
                 dma((7,)), dma((1,)), dma((5,)), dma((1,)), dma((1,)),
                 dma((1,)), dma((n_round,)), dma((1,)), dma((1,)), dma((n_round,)),
                 dma((3,)), dma((3,)), dma((4,)), dma((4,)), dma((1,)), dma((2,)), dma((1,)), dma((2,)), dma((1,)), dma((1,)),
-                pltpu.SemaphoreType.REGULAR((3,)),
+                pltpu.SemaphoreType.REGULAR((N_HOP,)),
                 pltpu.VMEM((rows, width), BF16),
                 pltpu.VMEM((1, rows), jnp.int32),
                 pltpu.VMEM((4, 1, width), F32),

time: 151 us -> 150 us (level)
  no operation moved by 1% of the time
where the time goes in v7:
time: 150 us
  Pallas kernels  150 us (100%)
    pallas_call x1, Pallas kernels, per_device(): pl.pallas_call(functools.partial(head_kernel, n_vp, n_tp, n_block, width...  148 us

profile of v7, /device:TPU:1, one launch (start us, length us, event | category | flops | bytes accessed | tf_op | source)
XLA Modules:
  0.0 150.3 jit_solution(7380135106517302451)
XLA Ops:
  0.6 147.6 %shard_map.94 = (f32[1960,512]{1,0:T(8,128)S(1)}, f32[1,512]{1,0:T(1,128)S(1)}, bf16[512,256]{1,0:T(8,128)(2,1)S(1)}) custom-call(bf16[512,256]{1,0:T(8,128)(2,1)} %hid_hbm.1, f32[1,256]{1,0:T(1,128)} %bitcast.10, f32[1,256]{1,0:T(1,128)} %bitcast.11, bf16[15680,256]{1,0:T(8,128)(2,1)} %emb_ref.1, s32[1,512]{1,0:T(1,128)} %bitcast.8, f32[1,256]{1,0:T(1,128)} %bitcast.12, ...), custom_call_target="tpu_custom_call" | custom-call | flops 8220835840 | bytes 64225280 | tf_op jit(solution)/shard_map/pallas_call | solution.py:569
  148.2 2.1 %shard_map.95 = (f32[1960,512]{1,0:T(8,128)}, f32[1,512]{1,0:T(1,128)}, bf16[512,256]{1,0:T(8,128)(2,1)}) custom-call(f32[1960,512]{1,0:T(8,128)S(1)} %get-tuple-element.9.z_ref, f32[1,512]{1,0:T(1,128)S(1)} %get-tuple-element.10.lse_ref, bf16[512,256]{1,0:T(8,128)(2,1)S(1)} %get-tuple-element.11.next_ref), custom_call_target="tpu_custom_call" | custom-call | tf_op jit(solution)/shard_map/pallas_call | solution.py:621

commit v8 on v7

--- a/solution.py
+++ b/solution.py
@@ -9,7 +9,7 @@
 
 NORM_EPS = 1e-5
 MESH = pl.DeviceIdType.MESH
-CHUNK = 128
+CHUNK = 144
 F32 = jnp.float32
 BF16 = jnp.bfloat16
 
@@ -73,7 +73,7 @@
         if isinstance(i, int) and i == 0:
             return (tail0, small1) if h == 0 else (tail0 + small1, small2)
         off = h * half * CHUNK + (i - 1) * CHUNK
-        return (off if isinstance(i, int) else pl.multiple_of(off, CHUNK)), CHUNK
+        return (off if isinstance(i, int) else pl.multiple_of(off, 16)), CHUNK
 
     barrier = pltpu.get_barrier_semaphore()
     for j in range(1, n_tp):
@@ -448,9 +448,9 @@
             gather(2 * i - 2)
             gather(2 * i - 1)
 
-        at(i, 2, slabs_swap)
-        at(i, 3, rows_scatter, slabs_done)
-        at(i, 4, rows_stats, settle_raw)
+        at(i, 3, rows_scatter)
+        at(i, 4, slabs_swap, rows_stats)
+        at(i, 5, slabs_done, settle_raw)
         at(i, 6, rows_norm)
 
         @pl.when(i >= 3)
@@ -478,22 +478,19 @@
 
     m8 = m_acc[...]
     top = jnp.max(m8, axis=0, keepdims=True)
-    mine = vp * 2 + core
-    st_all[mine] = top + jnp.log(jnp.sum(s_acc[...] * jnp.exp(m8 - top), axis=0, keepdims=True))
-
-    def collect(peer):
-        return pltpu.make_async_remote_copy(
-            src_ref=st_all.at[mine], dst_ref=st_all.at[mine], send_sem=v_send.at[2], recv_sem=v_recv.at[2],
-            device_id={"vp": peer, "tp": chip * 2 + 1}, device_id_type=MESH)
-
-    shifts = sorted(((dz, dy) for dz in range(n_z) for dy in range(SIDE) if dz or dy),
-                    key=lambda d: -min(d[0], n_z - d[0]) - min(d[1], SIDE - d[1]))
-    for dz, dy in shifts:
-        collect(lax.rem(z + dz, n_z) * SIDE + lax.rem(y + dy, SIDE)).start()
+    st_lse[tp] = top + jnp.log(jnp.sum(s_acc[...] * jnp.exp(m8 - top), axis=0, keepdims=True))
+
+    def collect(to_chip):
+        return pltpu.make_async_remote_copy(
+            src_ref=st_lse.at[tp], dst_ref=st_lse.at[tp], send_sem=t_send.at[2], recv_sem=t_recv.at[2],
+            device_id={"tp": to_chip * 2 + 1}, device_id_type=MESH)
+
+    for j in (2, 3, 1):
+        collect(lax.rem(chip + j, n_chip)).start()
 
     @pl.when(core == 0)
     def _():
-        collect(vp).start()
+        collect(chip).start()
 
     rows_out()
     hx_copy.wait_send()
@@ -514,24 +511,35 @@
     vp_drain(rs_buf, 0)
     vp_drain(ag_buf, 1)
 
+    def spread(to_vp, to_tp):
+        return pltpu.make_async_remote_copy(
+            src_ref=st_all.at[vp], dst_ref=st_all.at[vp], send_sem=v_send.at[2], recv_sem=v_recv.at[2],
+            device_id={"vp": to_vp, "tp": to_tp}, device_id_type=MESH)
+
+    shifts = sorted(((dz, dy) for dz in range(n_z) for dy in range(SIDE) if dz or dy),
+                    key=lambda d: -min(d[0], n_z - d[0]) - min(d[1], SIDE - d[1]))
+
     @pl.when(core == 1)
     def _():
-        total_recv(st_all.at[pl.ds(0, 2 * n_vp - 1)], v_recv.at[2])
-        st_lse[chip] = merge(st_all, 2 * n_vp)
-        for peer in [lax.rem(tp + j, n_tp) for j in (3, 4, 1, 2, 5, 6, 7)]:
-            pltpu.make_async_remote_copy(
-                src_ref=st_lse.at[chip], dst_ref=st_lse.at[chip], send_sem=t_send.at[2], recv_sem=t_recv.at[2],
-                device_id={"tp": peer}, device_id_type=MESH).start()
-        total_send(st_all.at[pl.ds(0, n_vp - 1)], v_send.at[2])
-        total_recv(st_lse.at[pl.ds(0, n_chip - 1)], t_recv.at[2])
-        total_send(st_all.at[pl.ds(0, n_tp - 1)], t_send.at[2])
+        total_recv(st_lse.at[pl.ds(0, n_tp - 1)], t_recv.at[2])
+        st_all[vp] = merge(st_lse, n_tp)
+        for dz, dy in shifts:
+            for to_tp in (tp - 1, tp):
+                spread(lax.rem(z + dz, n_z) * SIDE + lax.rem(y + dy, SIDE), to_tp).start()
+        spread(vp, tp - 1).start()
+        total_send(st_lse.at[pl.ds(0, n_chip - 1)], t_send.at[2])
+        total_recv(st_all.at[pl.ds(0, n_vp - 1)], v_recv.at[2])
 
     @pl.when(core == 0)
     def _():
-        total_send(st_all.at[pl.ds(0, n_vp)], v_send.at[2])
-        total_recv(st_lse, t_recv.at[2])
-
-    lse_ref[...] = merge(st_lse, n_chip)
+        total_send(st_lse.at[pl.ds(0, n_chip)], t_send.at[2])
+        total_recv(st_all.at[pl.ds(0, n_vp)], v_recv.at[2])
+
+    lse_ref[...] = merge(st_all, n_vp)
+
+    @pl.when(core == 1)
+    def _():
+        total_send(st_all.at[pl.ds(0, 2 * n_vp - 1)], v_send.at[2])
 
 
 def finish_kernel(n_piece, z_ref, lse_ref, next_ref, out_ref, sum_ref, row_ref, buf, sems):
@@ -591,7 +599,7 @@
                 pltpu.VMEM((8, rows), F32),
                 pltpu.VMEM((rows, width), F32),
                 pltpu.VMEM((n_tp, 1, 2 * rows), F32),
-                pltpu.VMEM((n_tp // 2, 1, rows), F32),
+                pltpu.VMEM((n_tp, 1, rows), F32),
                 pltpu.VMEM((2 * n_vp, 1, rows), F32),
                 pltpu.VMEM((n_vp, slab, width), F32),
                 pltpu.VMEM((n_tp, 1, 256), F32),

time: 150 us -> 150 us (level)
  no operation moved by 1% of the time
where the time goes in v8:
time: 150 us
  Pallas kernels  150 us (100%)
    pallas_call x1, Pallas kernels, per_device(): pl.pallas_call(functools.partial(head_kernel, n_vp, n_tp, n_block, width...  148 us

profile of v8, /device:TPU:1, one launch (start us, length us, event | category | flops | bytes accessed | tf_op | source)
XLA Modules:
  0.0 150.3 jit_solution(1976305758847767207)
XLA Ops:
  0.6 147.6 %shard_map.94 = (f32[1960,512]{1,0:T(8,128)S(1)}, f32[1,512]{1,0:T(1,128)S(1)}, bf16[512,256]{1,0:T(8,128)(2,1)S(1)}) custom-call(bf16[512,256]{1,0:T(8,128)(2,1)} %hid_hbm.1, f32[1,256]{1,0:T(1,128)} %bitcast.10, f32[1,256]{1,0:T(1,128)} %bitcast.11, bf16[15680,256]{1,0:T(8,128)(2,1)} %emb_ref.1, s32[1,512]{1,0:T(1,128)} %bitcast.8, f32[1,256]{1,0:T(1,128)} %bitcast.12, ...), custom_call_target="tpu_custom_call" | custom-call | flops 8220835840 | bytes 64225280 | tf_op jit(solution)/shard_map/pallas_call | solution.py:577
  148.2 2.1 %shard_map.95 = (f32[1960,512]{1,0:T(8,128)}, f32[1,512]{1,0:T(1,128)}, bf16[512,256]{1,0:T(8,128)(2,1)}) custom-call(f32[1960,512]{1,0:T(8,128)S(1)} %get-tuple-element.9.z_ref, f32[1,512]{1,0:T(1,128)S(1)} %get-tuple-element.10.lse_ref, bf16[512,256]{1,0:T(8,128)(2,1)S(1)} %get-tuple-element.11.next_ref), custom_call_target="tpu_custom_call" | custom-call | tf_op jit(solution)/shard_map/pallas_call | solution.py:629

commit v9 on v8

--- a/solution.py
+++ b/solution.py
@@ -16,6 +16,7 @@
 OPP, LEFT, RIGHT, OWN = 0, 1, 2, 3
 SIDE = 4
 N_HOP = 5
+FIRST = 1
 STEP_OF_SLOT = (2, 3, 1, 0)
 
 
@@ -23,11 +24,11 @@
                 hid_hbm, g_hbm, b_hbm, emb_ref, tok_hbm, eg_hbm, eb_hbm,
                 logits_ref, lse_ref, next_ref,
                 e_own, e_oth, e_out, e_in, send_f, recv_f, send_n, recv_l, recv_r,
-                hx, xn, m_acc, s_acc, pick, st_ln, st_lse, st_all, rs_buf, row_st, ag_buf,
+                hx, xn, m_acc, s_acc, pick, st_ln, st_lse, st_all, rs_buf, row_st, ag_buf, st_dir,
                 raw_src, raw_l, raw_r, slab_src, nb, nb_par, xnb,
                 ld_sem, ex_send, ex_recv, hx_send, hx_recv,
                 f_send, f_recv, n_send, r_send, in_recv,
-                t_send, t_recv, v_send, v_recv, raw_send, raw_recv, sx_send, sx_recv, nb_send, nb_recv, hop,
+                t_send, t_recv, v_send, v_recv, raw_send, raw_recv, sx_recv, nb_recv, d_recv, hop,
                 hid_ref, tok_ref, vec_ref, in_sem):
     vp = lax.axis_index("vp")
     tp = lax.axis_index("tp")
@@ -146,14 +147,14 @@
     def tp_start(buf, stage):
         for j in range(1, n_tp):
             pltpu.make_async_remote_copy(
-                src_ref=buf.at[tp], dst_ref=buf.at[tp], send_sem=t_send.at[stage], recv_sem=t_recv.at[stage],
+                src_ref=buf.at[tp], dst_ref=buf.at[tp], send_sem=t_send.at[0], recv_sem=t_recv.at[stage],
                 device_id={"tp": lax.rem(tp + j, n_tp)}, device_id_type=MESH).start()
 
     def tp_wait(buf, stage):
         total_recv(buf.at[pl.ds(0, n_tp - 1)], t_recv.at[stage])
 
-    def tp_drain(buf, stage):
-        total_send(buf.at[pl.ds(0, n_tp - 1)], t_send.at[stage])
+    def tp_drain(buf):
+        total_send(buf.at[pl.ds(0, n_tp - 1)], t_send.at[0])
 
     tp_start(st_ln, 0)
     for other in (False, True):
@@ -207,9 +208,10 @@
     def slab_copy(d):
         return pltpu.make_async_remote_copy(
             src_ref=slab_src, dst_ref=nb.at[d, pl.ds(pl.multiple_of(vp * xslab, 8), xslab), :],
-            send_sem=sx_send.at[0], recv_sem=sx_recv.at[d], device_id=right if d == 0 else left, device_id_type=MESH)
+            send_sem=hx_send.at[0], recv_sem=sx_recv.at[d], device_id=right if d == 0 else left, device_id_type=MESH)
 
     norm(0)
+    hx_copy.wait_send()
 
     @pl.when(carries)
     def _():
@@ -326,7 +328,7 @@
 
     def v_copy(src, dst, stage, j):
         return pltpu.make_async_remote_copy(
-            src_ref=src, dst_ref=dst, send_sem=v_send.at[stage], recv_sem=v_recv.at[stage],
+            src_ref=src, dst_ref=dst, send_sem=v_send.at[0], recv_sem=v_recv.at[stage],
             device_id={"vp": lax.rem(vp + j, n_vp)}, device_id_type=MESH)
 
     def vp_start(buf, stage):
@@ -336,8 +338,8 @@
     def vp_wait(buf, stage):
         total_recv(buf.at[pl.ds(0, n_vp - 1)], v_recv.at[stage])
 
-    def vp_drain(buf, stage):
-        total_send(buf.at[pl.ds(0, n_vp - 1)], v_send.at[stage])
+    def vp_drain(buf):
+        total_send(buf.at[pl.ds(0, n_vp - 1)], v_send.at[0])
 
     def slabs_forward():
         hear_near(N_HOP - 1)
@@ -351,11 +353,12 @@
                     v_copy(nb.at[d, own, :], nb.at[d, own, :], 3, j).start()
 
     nb_copy = pltpu.make_async_remote_copy(
-        src_ref=nb, dst_ref=nb_par, send_sem=nb_send.at[0], recv_sem=nb_recv.at[0], device_id=partner, device_id_type=MESH)
+        src_ref=nb, dst_ref=nb_par, send_sem=hx_send.at[0], recv_sem=nb_recv.at[0], device_id=partner, device_id_type=MESH)
 
     def slabs_swap():
         @pl.when(carries)
         def _():
+            total_send(nb.at[0, pl.ds(0, 2 * xslab), :], hx_send.at[0])
             total_recv(nb.at[:, pl.ds(0, width - xslab), :], v_recv.at[3])
 
         @pl.when(jnp.logical_not(carries))
@@ -372,6 +375,10 @@
             xnb[d, 1] = nb_par[d].astype(BF16)
 
     def rows_scatter():
+        @pl.when(carries)
+        def _():
+            total_send(send_f.at[pl.ds(0, 2 * (n_vp - 1) * xslab), :], v_send.at[0])
+
         for j in range(1, n_vp):
             peer = lax.rem(vp + j, n_vp)
             v_copy(pick.at[pl.ds(pl.multiple_of(peer * slab, 8), slab), :], rs_buf.at[vp], 0, j).start()
@@ -385,6 +392,7 @@
         ag_buf[vp] = tot
         lane = lax.broadcasted_iota(jnp.int32, (slab, 128), 1)
         both = jnp.where(lane == 0, jnp.sum(tot, axis=1, keepdims=True), jnp.sum(tot * tot, axis=1, keepdims=True)).T
+        tp_drain(st_ln)
         row_st[tp] = jnp.zeros((1, 256), F32)
         row_st[tp, :, 0:slab] = both[0:1]
         row_st[tp, :, 128:128 + slab] = both[1:2]
@@ -392,6 +400,7 @@
 
     def rows_norm():
         tp_wait(row_st, 1)
+        tp_drain(row_st)
         tot = row_st[0]
         for j in range(1, n_tp):
             tot = tot + row_st[j]
@@ -401,6 +410,7 @@
         rs = jnp.broadcast_to(rs, (128, 128)).T[0:slab, 0:1]
         out = ((ag_buf[vp] - mu) * rs * vec_ref[2] + vec_ref[3]).astype(BF16)
         ag_buf[vp] = out.astype(F32)
+        vp_drain(rs_buf)
         vp_start(ag_buf, 1)
 
     def rows_out():
@@ -427,6 +437,9 @@
     load(OWN, False, 2, 6).wait()
     ex_copy(OWN, 2, 4).wait_recv()
 
+    def raw_drain():
+        total_send(e_in.at[0, pl.ds(0, 2 * small), :], raw_send.at[0])
+
     def at(i, when, *steps):
         @pl.when(i == when)
         def _():
@@ -441,7 +454,7 @@
             far(i + 2)
 
         relay(i)
-        at(i, 1, slabs_forward)
+        at(i, 1, slabs_forward, raw_drain)
 
         @pl.when(i <= 2)
         def _():
@@ -468,78 +481,100 @@
     lax.fori_loop(n_round - 2, n_round, last_body, 0)
 
     def merge(buf, n):
-        top = buf[0]
-        for j in range(1, n):
-            top = jnp.maximum(top, buf[j])
-        tot = jnp.exp(buf[0] - top)
-        for j in range(1, n):
-            tot = tot + jnp.exp(buf[j] - top)
-        return top + jnp.log(tot)
+        sums = buf[0:n]
+        top = jnp.max(sums, axis=0)
+        return top + jnp.log(jnp.sum(jnp.exp(sums - top[None]), axis=0))
+
+    def put(dst, at, value):
+        for k in range(rows // 128):
+            dst[at, k:k + 1, :] = value[:, k * 128:k * 128 + 128]
 
     m8 = m_acc[...]
     top = jnp.max(m8, axis=0, keepdims=True)
-    st_lse[tp] = top + jnp.log(jnp.sum(s_acc[...] * jnp.exp(m8 - top), axis=0, keepdims=True))
+    put(st_lse, tp, top + jnp.log(jnp.sum(s_acc[...] * jnp.exp(m8 - top), axis=0, keepdims=True)))
+
+    me = vp * n_tp + tp
+    is_first = me == FIRST
+
+    @pl.when(jnp.logical_not(is_first))
+    def _():
+        pltpu.make_async_remote_copy(
+            src_ref=st_lse.at[tp], dst_ref=st_dir.at[me], send_sem=raw_send.at[0], recv_sem=d_recv.at[0],
+            device_id={"vp": FIRST // n_tp, "tp": FIRST % n_tp}, device_id_type=MESH).start()
 
     def collect(to_chip):
         return pltpu.make_async_remote_copy(
-            src_ref=st_lse.at[tp], dst_ref=st_lse.at[tp], send_sem=t_send.at[2], recv_sem=t_recv.at[2],
+            src_ref=st_lse.at[tp], dst_ref=st_lse.at[tp], send_sem=t_send.at[0], recv_sem=t_recv.at[2],
             device_id={"tp": to_chip * 2 + 1}, device_id_type=MESH)
 
-    for j in (2, 3, 1):
-        collect(lax.rem(chip + j, n_chip)).start()
-
-    @pl.when(core == 0)
-    def _():
-        collect(chip).start()
+    for to in range(n_chip):
+        @pl.when(jnp.logical_or(chip != to, core == 0))
+        def _(to=to):
+            collect(to).start()
 
     rows_out()
-    hx_copy.wait_send()
     nb_copy.wait_send()
     total_send(e_out, ex_send.at[0])
-    total_send(e_in.at[0, pl.ds(0, 2 * small), :], raw_send.at[0])
-
-    @pl.when(carries)
-    def _():
-        total_send(nb.at[0, pl.ds(0, 2 * xslab), :], sx_send.at[0])
-        total_send(send_f.at[pl.ds(0, 2 * (n_vp - 1) * xslab), :], v_send.at[3])
-
     total_send(send_f, f_send.at[0])
     total_send(recv_f, r_send.at[0])
     total_send(send_n.at[pl.ds(0, tail0), :], n_send.at[0])
-    tp_drain(st_ln, 0)
-    tp_drain(row_st, 1)
-    vp_drain(rs_buf, 0)
-    vp_drain(ag_buf, 1)
-
-    def spread(to_vp, to_tp):
-        return pltpu.make_async_remote_copy(
-            src_ref=st_all.at[vp], dst_ref=st_all.at[vp], send_sem=v_send.at[2], recv_sem=v_recv.at[2],
-            device_id={"vp": to_vp, "tp": to_tp}, device_id_type=MESH)
-
-    shifts = sorted(((dz, dy) for dz in range(n_z) for dy in range(SIDE) if dz or dy),
-                    key=lambda d: -min(d[0], n_z - d[0]) - min(d[1], SIDE - d[1]))
+    vp_drain(ag_buf)
+
+    def spread(to, to_core):
+        return pltpu.make_async_remote_copy(
+            src_ref=st_all.at[vp], dst_ref=st_all.at[vp], send_sem=v_send.at[0], recv_sem=v_recv.at[2],
+            device_id={"vp": to, "tp": chip * 2 + to_core}, device_id_type=MESH)
+
+    def is_first_at(to, to_core):
+        return jnp.logical_and(to == FIRST // n_tp, chip * 2 + to_core == FIRST % n_tp)
 
     @pl.when(core == 1)
     def _():
         total_recv(st_lse.at[pl.ds(0, n_tp - 1)], t_recv.at[2])
         st_all[vp] = merge(st_lse, n_tp)
-        for dz, dy in shifts:
-            for to_tp in (tp - 1, tp):
-                spread(lax.rem(z + dz, n_z) * SIDE + lax.rem(y + dy, SIDE), to_tp).start()
-        spread(vp, tp - 1).start()
-        total_send(st_lse.at[pl.ds(0, n_chip - 1)], t_send.at[2])
-        total_recv(st_all.at[pl.ds(0, n_vp - 1)], v_recv.at[2])
+        for to in range(n_vp):
+            @pl.when(jnp.logical_and(vp != to, jnp.logical_not(is_first_at(to, 1))))
+            def _(to=to):
+                spread(to, 1).start()
+        for to in range(n_vp):
+            spread(to, 0).start()
+        total_send(st_lse.at[pl.ds(0, n_chip - 1)], t_send.at[0])
+
+        @pl.when(jnp.logical_not(is_first))
+        def _():
+            total_recv(st_all.at[pl.ds(0, n_vp - 1)], v_recv.at[2])
 
     @pl.when(core == 0)
     def _():
-        total_send(st_lse.at[pl.ds(0, n_chip)], t_send.at[2])
+        total_send(st_lse.at[pl.ds(0, n_chip)], t_send.at[0])
         total_recv(st_all.at[pl.ds(0, n_vp)], v_recv.at[2])
 
-    lse_ref[...] = merge(st_all, n_vp)
-
-    @pl.when(core == 1)
-    def _():
-        total_send(st_all.at[pl.ds(0, 2 * n_vp - 1)], v_send.at[2])
+    def result(value):
+        for k in range(rows // 128):
+            lse_ref[:, k * 128:k * 128 + 128] = value[k:k + 1, :]
+
+    @pl.when(is_first)
+    def _():
+        put_row = st_lse[tp]
+        st_dir[me] = put_row
+        total_recv(st_dir.at[pl.ds(0, n_vp * n_tp - 1)], d_recv.at[0])
+        result(merge(st_dir, n_vp * n_tp))
+
+    @pl.when(jnp.logical_not(is_first))
+    def _():
+        result(merge(st_all, n_vp))
+        total_send(st_lse.at[pl.ds(0, 1)], raw_send.at[0])
+
+    sends = 2 * n_vp - 1
+    short = jnp.logical_and(chip == FIRST % n_tp // 2, vp != FIRST // n_tp)
+
+    @pl.when(jnp.logical_and(core == 1, short))
+    def _():
+        total_send(st_all.at[pl.ds(0, sends - 1)], v_send.at[0])
+
+    @pl.when(jnp.logical_and(core == 1, jnp.logical_not(short)))
+    def _():
+        total_send(st_all.at[pl.ds(0, sends)], v_send.at[0])
 
 
 def finish_kernel(n_piece, z_ref, lse_ref, next_ref, out_ref, sum_ref, row_ref, buf, sems):
@@ -599,11 +634,12 @@
                 pltpu.VMEM((8, rows), F32),
                 pltpu.VMEM((rows, width), F32),
                 pltpu.VMEM((n_tp, 1, 2 * rows), F32),
-                pltpu.VMEM((n_tp, 1, rows), F32),
-                pltpu.VMEM((2 * n_vp, 1, rows), F32),
+                pltpu.VMEM((n_tp, rows // 128, 128), F32),
+                pltpu.VMEM((2 * n_vp, rows // 128, 128), F32),
                 pltpu.VMEM((n_vp, slab, width), F32),
                 pltpu.VMEM((n_tp, 1, 256), F32),
                 pltpu.VMEM((n_vp, slab, width), F32),
+                pltpu.VMEM((n_vp * n_tp, rows // 128, 128), F32),
                 pltpu.VMEM((small, width), F32),
                 pltpu.VMEM((2, small // 16 * 8, width), F32),
                 pltpu.VMEM((2, small - small // 16 * 8, width), F32),
@@ -613,7 +649,7 @@
                 pltpu.VMEM((2, 2, width, rows), BF16),
                 dma((7,)), dma((1,)), dma((5,)), dma((1,)), dma((1,)),
                 dma((1,)), dma((n_round,)), dma((1,)), dma((1,)), dma((n_round,)),
-                dma((3,)), dma((3,)), dma((4,)), dma((4,)), dma((1,)), dma((2,)), dma((1,)), dma((2,)), dma((1,)), dma((1,)),
+                dma((1,)), dma((3,)), dma((1,)), dma((4,)), dma((1,)), dma((2,)), dma((2,)), dma((1,)), dma((1,)),
                 pltpu.SemaphoreType.REGULAR((N_HOP,)),
                 pltpu.VMEM((rows, width), BF16),
                 pltpu.VMEM((1, rows), jnp.int32),

time: 150 us -> 150 us (level); the launches traced: 150 us -> 149 us
  Pallas kernels: 150 us -> 148 us
    pallas_call x1, Pallas kernels: 148 us -> 146 us  [per_device(): pl.pallas_call(functools.partial(head_kernel, n_vp, n_tp, n_block, width...]
where the time goes in v9:
time: 150 us; the launch traced here: 149 us
  Pallas kernels  148 us (99%)
    pallas_call x1, Pallas kernels, per_device(): pl.pallas_call(functools.partial(head_kernel, n_vp, n_tp, n_block, width...  146 us

profile of v9, /device:TPU:1, one launch (start us, length us, event | category | flops | bytes accessed | tf_op | source)
XLA Modules:
  0.0 148.8 jit_solution(5459657271777241198)
XLA Ops:
  0.6 146.0 %shard_map.94 = (f32[1960,512]{1,0:T(8,128)S(1)}, f32[1,512]{1,0:T(1,128)S(1)}, bf16[512,256]{1,0:T(8,128)(2,1)S(1)}) custom-call(bf16[512,256]{1,0:T(8,128)(2,1)} %hid_hbm.1, f32[1,256]{1,0:T(1,128)} %bitcast.10, f32[1,256]{1,0:T(1,128)} %bitcast.11, bf16[15680,256]{1,0:T(8,128)(2,1)} %emb_ref.1, s32[1,512]{1,0:T(1,128)} %bitcast.8, f32[1,256]{1,0:T(1,128)} %bitcast.12, ...), custom_call_target="tpu_custom_call" | custom-call | flops 8220835840 | bytes 64225280 | tf_op jit(solution)/shard_map/pallas_call | solution.py:612
  146.7 2.1 %shard_map.95 = (f32[1960,512]{1,0:T(8,128)}, f32[1,512]{1,0:T(1,128)}, bf16[512,256]{1,0:T(8,128)(2,1)}) custom-call(f32[1960,512]{1,0:T(8,128)S(1)} %get-tuple-element.9.z_ref, f32[1,512]{1,0:T(1,128)S(1)} %get-tuple-element.10.lse_ref, bf16[512,256]{1,0:T(8,128)(2,1)S(1)} %get-tuple-element.11.next_ref), custom_call_target="tpu_custom_call" | custom-call | tf_op jit(solution)/shard_map/pallas_call | solution.py:665

commit v10 on v9

--- a/solution.py
+++ b/solution.py
@@ -10,6 +10,7 @@
 NORM_EPS = 1e-5
 MESH = pl.DeviceIdType.MESH
 CHUNK = 144
+LANE = 128
 F32 = jnp.float32
 BF16 = jnp.bfloat16
 
@@ -139,7 +140,7 @@
         to = (right_chip if slot == RIGHT else left_chip) * 2 + (1 - core if other else core)
         return pltpu.make_async_remote_copy(
             src_ref=src, dst_ref=(raw_l if slot == RIGHT else raw_r).at[int(other)],
-            send_sem=raw_send.at[0], recv_sem=raw_recv.at[int(slot == LEFT)],
+            send_sem=raw_send, recv_sem=raw_recv.at[int(slot == LEFT)],
             device_id={"tp": to}, device_id_type=MESH)
 
     pl.semaphore_wait(barrier, n_tp - 1 + n_near)
@@ -147,14 +148,14 @@
     def tp_start(buf, stage):
         for j in range(1, n_tp):
             pltpu.make_async_remote_copy(
-                src_ref=buf.at[tp], dst_ref=buf.at[tp], send_sem=t_send.at[0], recv_sem=t_recv.at[stage],
+                src_ref=buf.at[tp], dst_ref=buf.at[tp], send_sem=t_send, recv_sem=t_recv.at[stage],
                 device_id={"tp": lax.rem(tp + j, n_tp)}, device_id_type=MESH).start()
 
     def tp_wait(buf, stage):
         total_recv(buf.at[pl.ds(0, n_tp - 1)], t_recv.at[stage])
 
     def tp_drain(buf):
-        total_send(buf.at[pl.ds(0, n_tp - 1)], t_send.at[0])
+        total_send(buf.at[pl.ds(0, n_tp - 1)], t_send)
 
     tp_start(st_ln, 0)
     for other in (False, True):
@@ -162,10 +163,10 @@
             raw_copy(slot, other).start()
 
     total_load(vec_ref, in_sem.at[2])
-    hx[0, :, rows:rows + 128] = jnp.broadcast_to(vec_ref[0], (128, width)).T
-    hx[0, :, rows + 128:rows + 256] = jnp.broadcast_to(vec_ref[1], (128, width)).T
+    hx[0, :, rows:rows + LANE] = jnp.broadcast_to(vec_ref[0], (LANE, width)).T
+    hx[0, :, rows + LANE:rows + 256] = jnp.broadcast_to(vec_ref[1], (LANE, width)).T
     hx_copy = pltpu.make_async_remote_copy(
-        src_ref=hx.at[0], dst_ref=hx.at[1], send_sem=hx_send.at[0], recv_sem=hx_recv.at[0],
+        src_ref=hx.at[0], dst_ref=hx.at[1], send_sem=hx_send, recv_sem=hx_recv,
         device_id=partner, device_id_type=MESH)
     hx_copy.start()
     tell_near(hop.at[0])
@@ -174,7 +175,7 @@
         off, n = parts[q]
         return pltpu.make_async_remote_copy(
             src_ref=e_out.at[slot, pl.ds(off, n), :], dst_ref=e_in.at[slot, pl.ds(off, n), :],
-            send_sem=ex_send.at[0], recv_sem=ex_recv.at[sem], device_id=partner, device_id_type=MESH)
+            send_sem=ex_send, recv_sem=ex_recv.at[sem], device_id=partner, device_id_type=MESH)
 
     load(OPP, True, 2, 1).wait()
     for q in range(2):
@@ -199,16 +200,16 @@
     rstd = lax.rsqrt(total[:, rows:2 * rows] / full_width - mean * mean + NORM_EPS)
 
     def norm(which):
-        gain = hx[which, :, rows:rows + 128]
-        bias = hx[which, :, rows + 128:rows + 256]
-        for c in range(rows // 128):
-            cols = slice(c * 128, c * 128 + 128)
+        gain = hx[which, :, rows:rows + LANE]
+        bias = hx[which, :, rows + LANE:rows + 256]
+        for c in range(rows // LANE):
+            cols = slice(c * LANE, c * LANE + LANE)
             xn[which, :, cols] = ((hx[which, :, cols] - mean[:, cols]) * rstd[:, cols] * gain + bias).astype(BF16)
 
     def slab_copy(d):
         return pltpu.make_async_remote_copy(
             src_ref=slab_src, dst_ref=nb.at[d, pl.ds(pl.multiple_of(vp * xslab, 8), xslab), :],
-            send_sem=hx_send.at[0], recv_sem=sx_recv.at[d], device_id=right if d == 0 else left, device_id_type=MESH)
+            send_sem=hx_send, recv_sem=sx_recv.at[d], device_id=right if d == 0 else left, device_id_type=MESH)
 
     norm(0)
     hx_copy.wait_send()
@@ -232,7 +233,7 @@
         off, n = piece(h, i)
         return pltpu.make_async_remote_copy(
             src_ref=send_f.at[pl.ds(off, n), :], dst_ref=recv_f.at[pl.ds(off, n), :],
-            send_sem=f_send.at[0], recv_sem=f_recv.at[i],
+            send_sem=f_send, recv_sem=f_recv.at[i],
             device_id=left if h == 0 else right, device_id_type=MESH)
 
     def r_copy(h, i):
@@ -240,7 +241,7 @@
         dst = (recv_r if h == 0 else recv_l).at[pl.ds(off, n), :]
         return pltpu.make_async_remote_copy(
             src_ref=recv_f.at[pl.ds(off, n), :], dst_ref=dst,
-            send_sem=r_send.at[0], recv_sem=in_recv.at[i],
+            send_sem=r_send, recv_sem=in_recv.at[i],
             device_id=left if h == 0 else right, device_id_type=MESH)
 
     def n_copy(h, i):
@@ -248,7 +249,7 @@
         dst = (recv_l if h == 0 else recv_r).at[pl.ds(off, n), :]
         return pltpu.make_async_remote_copy(
             src_ref=send_n.at[pl.ds(off, n), :], dst_ref=dst,
-            send_sem=n_send.at[0], recv_sem=in_recv.at[i],
+            send_sem=n_send, recv_sem=in_recv.at[i],
             device_id=right if h == 0 else left, device_id_type=MESH)
 
     def far(i):
@@ -302,7 +303,7 @@
             logits_ref[pl.ds(off, n), :] = z
 
     tok_copy.wait()
-    tok = jnp.broadcast_to(tok_ref[...], (128, rows)).T
+    tok = jnp.broadcast_to(tok_ref[...], (LANE, rows)).T
 
     def gather(step):
         for other in range(2):
@@ -314,12 +315,12 @@
             acc = pick[...]
             for off in range(0, n_block, 512):
                 n = min(512, n_block - off)
-                for o, k in ((off, n // 128 * 128), (off + n // 128 * 128, n % 128)):
+                for o, k in ((off, n // LANE * LANE), (off + n // LANE * LANE, n % LANE)):
                     if k == 0:
                         continue
                     lane = lax.broadcasted_iota(jnp.int32, (rows, k), 1) + (base + o)
-                    if k % 128 == 0:
-                        want = jnp.concatenate([tok] * (k // 128), axis=1) if k > 128 else tok
+                    if k % LANE == 0:
+                        want = jnp.concatenate([tok] * (k // LANE), axis=1) if k > LANE else tok
                     else:
                         want = tok[:, :k]
                     hot = jnp.where(want == lane, 1.0, 0.0).astype(BF16)
@@ -328,7 +329,7 @@
 
     def v_copy(src, dst, stage, j):
         return pltpu.make_async_remote_copy(
-            src_ref=src, dst_ref=dst, send_sem=v_send.at[0], recv_sem=v_recv.at[stage],
+            src_ref=src, dst_ref=dst, send_sem=v_send, recv_sem=v_recv.at[stage],
             device_id={"vp": lax.rem(vp + j, n_vp)}, device_id_type=MESH)
 
     def vp_start(buf, stage):
@@ -339,7 +340,7 @@
         total_recv(buf.at[pl.ds(0, n_vp - 1)], v_recv.at[stage])
 
     def vp_drain(buf):
-        total_send(buf.at[pl.ds(0, n_vp - 1)], v_send.at[0])
+        total_send(buf.at[pl.ds(0, n_vp - 1)], v_send)
 
     def slabs_forward():
         hear_near(N_HOP - 1)
@@ -353,12 +354,12 @@
                     v_copy(nb.at[d, own, :], nb.at[d, own, :], 3, j).start()
 
     nb_copy = pltpu.make_async_remote_copy(
-        src_ref=nb, dst_ref=nb_par, send_sem=hx_send.at[0], recv_sem=nb_recv.at[0], device_id=partner, device_id_type=MESH)
+        src_ref=nb, dst_ref=nb_par, send_sem=hx_send, recv_sem=nb_recv, device_id=partner, device_id_type=MESH)
 
     def slabs_swap():
         @pl.when(carries)
         def _():
-            total_send(nb.at[0, pl.ds(0, 2 * xslab), :], hx_send.at[0])
+            total_send(nb.at[0, pl.ds(0, 2 * xslab), :], hx_send)
             total_recv(nb.at[:, pl.ds(0, width - xslab), :], v_recv.at[3])
 
         @pl.when(jnp.logical_not(carries))
@@ -377,7 +378,7 @@
     def rows_scatter():
         @pl.when(carries)
         def _():
-            total_send(send_f.at[pl.ds(0, 2 * (n_vp - 1) * xslab), :], v_send.at[0])
+            total_send(send_f.at[pl.ds(0, 2 * (n_vp - 1) * xslab), :], v_send)
 
         for j in range(1, n_vp):
             peer = lax.rem(vp + j, n_vp)
@@ -390,12 +391,12 @@
         for j in range(1, n_vp):
             tot = tot + rs_buf[j]
         ag_buf[vp] = tot
-        lane = lax.broadcasted_iota(jnp.int32, (slab, 128), 1)
+        lane = lax.broadcasted_iota(jnp.int32, (slab, LANE), 1)
         both = jnp.where(lane == 0, jnp.sum(tot, axis=1, keepdims=True), jnp.sum(tot * tot, axis=1, keepdims=True)).T
         tp_drain(st_ln)
         row_st[tp] = jnp.zeros((1, 256), F32)
         row_st[tp, :, 0:slab] = both[0:1]
-        row_st[tp, :, 128:128 + slab] = both[1:2]
+        row_st[tp, :, LANE:LANE + slab] = both[1:2]
         tp_start(row_st, 1)
 
     def rows_norm():
@@ -404,10 +405,10 @@
         tot = row_st[0]
         for j in range(1, n_tp):
             tot = tot + row_st[j]
-        mu = tot[:, 0:128] / full_width
-        rs = lax.rsqrt(tot[:, 128:256] / full_width - mu * mu + NORM_EPS)
-        mu = jnp.broadcast_to(mu, (128, 128)).T[0:slab, 0:1]
-        rs = jnp.broadcast_to(rs, (128, 128)).T[0:slab, 0:1]
+        mu = tot[:, 0:LANE] / full_width
+        rs = lax.rsqrt(tot[:, LANE:256] / full_width - mu * mu + NORM_EPS)
+        mu = jnp.broadcast_to(mu, (LANE, LANE)).T[0:slab, 0:1]
+        rs = jnp.broadcast_to(rs, (LANE, LANE)).T[0:slab, 0:1]
         out = ((ag_buf[vp] - mu) * rs * vec_ref[2] + vec_ref[3]).astype(BF16)
         ag_buf[vp] = out.astype(F32)
         vp_drain(rs_buf)
@@ -438,7 +439,7 @@
     ex_copy(OWN, 2, 4).wait_recv()
 
     def raw_drain():
-        total_send(e_in.at[0, pl.ds(0, 2 * small), :], raw_send.at[0])
+        total_send(e_in.at[0, pl.ds(0, 2 * small), :], raw_send)
 
     def at(i, when, *steps):
         @pl.when(i == when)
@@ -486,8 +487,8 @@
         return top + jnp.log(jnp.sum(jnp.exp(sums - top[None]), axis=0))
 
     def put(dst, at, value):
-        for k in range(rows // 128):
-            dst[at, k:k + 1, :] = value[:, k * 128:k * 128 + 128]
+        for k in range(rows // LANE):
+            dst[at, k:k + 1, :] = value[:, k * LANE:k * LANE + LANE]
 
     m8 = m_acc[...]
     top = jnp.max(m8, axis=0, keepdims=True)
@@ -499,12 +500,12 @@
     @pl.when(jnp.logical_not(is_first))
     def _():
         pltpu.make_async_remote_copy(
-            src_ref=st_lse.at[tp], dst_ref=st_dir.at[me], send_sem=raw_send.at[0], recv_sem=d_recv.at[0],
+            src_ref=st_lse.at[tp], dst_ref=st_dir.at[me], send_sem=raw_send, recv_sem=d_recv,
             device_id={"vp": FIRST // n_tp, "tp": FIRST % n_tp}, device_id_type=MESH).start()
 
     def collect(to_chip):
         return pltpu.make_async_remote_copy(
-            src_ref=st_lse.at[tp], dst_ref=st_lse.at[tp], send_sem=t_send.at[0], recv_sem=t_recv.at[2],
+            src_ref=st_lse.at[tp], dst_ref=st_lse.at[tp], send_sem=t_send, recv_sem=t_recv.at[2],
             device_id={"tp": to_chip * 2 + 1}, device_id_type=MESH)
 
     for to in range(n_chip):
@@ -514,15 +515,15 @@
 
     rows_out()
     nb_copy.wait_send()
-    total_send(e_out, ex_send.at[0])
-    total_send(send_f, f_send.at[0])
-    total_send(recv_f, r_send.at[0])
-    total_send(send_n.at[pl.ds(0, tail0), :], n_send.at[0])
+    total_send(e_out, ex_send)
+    total_send(send_f, f_send)
+    total_send(recv_f, r_send)
+    total_send(send_n.at[pl.ds(0, tail0), :], n_send)
     vp_drain(ag_buf)
 
     def spread(to, to_core):
         return pltpu.make_async_remote_copy(
-            src_ref=st_all.at[vp], dst_ref=st_all.at[vp], send_sem=v_send.at[0], recv_sem=v_recv.at[2],
+            src_ref=st_all.at[vp], dst_ref=st_all.at[vp], send_sem=v_send, recv_sem=v_recv.at[2],
             device_id={"vp": to, "tp": chip * 2 + to_core}, device_id_type=MESH)
 
     def is_first_at(to, to_core):
@@ -538,7 +539,7 @@
                 spread(to, 1).start()
         for to in range(n_vp):
             spread(to, 0).start()
-        total_send(st_lse.at[pl.ds(0, n_chip - 1)], t_send.at[0])
+        total_send(st_lse.at[pl.ds(0, n_chip - 1)], t_send)
 
         @pl.when(jnp.logical_not(is_first))
         def _():
@@ -546,35 +547,35 @@
 
     @pl.when(core == 0)
     def _():
-        total_send(st_lse.at[pl.ds(0, n_chip)], t_send.at[0])
+        total_send(st_lse.at[pl.ds(0, n_chip)], t_send)
         total_recv(st_all.at[pl.ds(0, n_vp)], v_recv.at[2])
 
     def result(value):
-        for k in range(rows // 128):
-            lse_ref[:, k * 128:k * 128 + 128] = value[k:k + 1, :]
+        for k in range(rows // LANE):
+            lse_ref[:, k * LANE:k * LANE + LANE] = value[k:k + 1, :]
 
     @pl.when(is_first)
     def _():
         put_row = st_lse[tp]
         st_dir[me] = put_row
-        total_recv(st_dir.at[pl.ds(0, n_vp * n_tp - 1)], d_recv.at[0])
+        total_recv(st_dir.at[pl.ds(0, n_vp * n_tp - 1)], d_recv)
         result(merge(st_dir, n_vp * n_tp))
 
     @pl.when(jnp.logical_not(is_first))
     def _():
         result(merge(st_all, n_vp))
-        total_send(st_lse.at[pl.ds(0, 1)], raw_send.at[0])
+        total_send(st_lse.at[pl.ds(0, 1)], raw_send)
 
     sends = 2 * n_vp - 1
     short = jnp.logical_and(chip == FIRST % n_tp // 2, vp != FIRST // n_tp)
 
     @pl.when(jnp.logical_and(core == 1, short))
     def _():
-        total_send(st_all.at[pl.ds(0, sends - 1)], v_send.at[0])
+        total_send(st_all.at[pl.ds(0, sends - 1)], v_send)
 
     @pl.when(jnp.logical_and(core == 1, jnp.logical_not(short)))
     def _():
-        total_send(st_all.at[pl.ds(0, sends)], v_send.at[0])
+        total_send(st_all.at[pl.ds(0, sends)], v_send)
 
 
 def finish_kernel(n_piece, z_ref, lse_ref, next_ref, out_ref, sum_ref, row_ref, buf, sems):
@@ -619,27 +620,21 @@
             in_specs=[pl.BlockSpec(memory_space=pl.ANY)] * 7,
             out_specs=(vmem, vmem, vmem),
             scratch_shapes=[
-                pltpu.VMEM((4, n_block, width), BF16),
-                pltpu.VMEM((4, n_block, width), BF16),
-                pltpu.VMEM((4, n_block, width), F32),
-                pltpu.VMEM((4, n_block, width), F32),
-                pltpu.VMEM((n_block, rows), F32),
-                pltpu.VMEM((n_block, rows), F32),
-                pltpu.VMEM((n_block, rows), F32),
-                pltpu.VMEM((n_block, rows), F32),
-                pltpu.VMEM((n_block, rows), F32),
+                *[pltpu.VMEM((4, n_block, width), BF16)] * 2,
+                *[pltpu.VMEM((4, n_block, width), F32)] * 2,
+                *[pltpu.VMEM((n_block, rows), F32)] * 5,
                 pltpu.VMEM((2, width, rows + 256), F32),
                 pltpu.VMEM((2, width, rows), BF16),
                 pltpu.VMEM((8, rows), F32),
                 pltpu.VMEM((8, rows), F32),
                 pltpu.VMEM((rows, width), F32),
                 pltpu.VMEM((n_tp, 1, 2 * rows), F32),
-                pltpu.VMEM((n_tp, rows // 128, 128), F32),
-                pltpu.VMEM((2 * n_vp, rows // 128, 128), F32),
+                pltpu.VMEM((n_tp, rows // LANE, LANE), F32),
+                pltpu.VMEM((2 * n_vp, rows // LANE, LANE), F32),
                 pltpu.VMEM((n_vp, slab, width), F32),
                 pltpu.VMEM((n_tp, 1, 256), F32),
                 pltpu.VMEM((n_vp, slab, width), F32),
-                pltpu.VMEM((n_vp * n_tp, rows // 128, 128), F32),
+                pltpu.VMEM((n_vp * n_tp, rows // LANE, LANE), F32),
                 pltpu.VMEM((small, width), F32),
                 pltpu.VMEM((2, small // 16 * 8, width), F32),
                 pltpu.VMEM((2, small - small // 16 * 8, width), F32),
@@ -647,9 +642,9 @@
                 pltpu.VMEM((2, width, rows), F32),
                 pltpu.VMEM((2, width, rows), F32),
                 pltpu.VMEM((2, 2, width, rows), BF16),
-                dma((7,)), dma((1,)), dma((5,)), dma((1,)), dma((1,)),
-                dma((1,)), dma((n_round,)), dma((1,)), dma((1,)), dma((n_round,)),
-                dma((1,)), dma((3,)), dma((1,)), dma((4,)), dma((1,)), dma((2,)), dma((2,)), dma((1,)), dma((1,)),
+                dma((7,)), dma, dma((5,)), dma, dma,
+                dma, dma((n_round,)), dma, dma, dma((n_round,)),
+                dma, dma((3,)), dma, dma((4,)), dma, dma((2,)), dma((2,)), dma, dma,
                 pltpu.SemaphoreType.REGULAR((N_HOP,)),
                 pltpu.VMEM((rows, width), BF16),
                 pltpu.VMEM((1, rows), jnp.int32),

time: 150 us -> 150 us (level)
  no operation moved by 1% of the time
where the time goes in v10:
time: 150 us; the launch traced here: 149 us
  Pallas kernels  148 us (99%)
    pallas_call x1, Pallas kernels, per_device(): pl.pallas_call(functools.partial(head_kernel, n_vp, n_tp, n_block, width...  146 us

profile of v10, /device:TPU:1, one launch (start us, length us, event | category | flops | bytes accessed | tf_op | source)
XLA Modules:
  0.0 148.8 jit_solution(5459657271777241198)
XLA Ops:
  0.6 146.0 %shard_map.94 = (f32[1960,512]{1,0:T(8,128)S(1)}, f32[1,512]{1,0:T(1,128)S(1)}, bf16[512,256]{1,0:T(8,128)(2,1)S(1)}) custom-call(bf16[512,256]{1,0:T(8,128)(2,1)} %hid_hbm.1, f32[1,256]{1,0:T(1,128)} %bitcast.10, f32[1,256]{1,0:T(1,128)} %bitcast.11, bf16[15680,256]{1,0:T(8,128)(2,1)} %emb_ref.1, s32[1,512]{1,0:T(1,128)} %bitcast.8, f32[1,256]{1,0:T(1,128)} %bitcast.12, ...), custom_call_target="tpu_custom_call" | custom-call | flops 8220835840 | bytes 64225280 | tf_op jit(solution)/shard_map/pallas_call | solution.py:613
  146.7 2.1 %shard_map.95 = (f32[1960,512]{1,0:T(8,128)}, f32[1,512]{1,0:T(1,128)}, bf16[512,256]{1,0:T(8,128)(2,1)}) custom-call(f32[1960,512]{1,0:T(8,128)S(1)} %get-tuple-element.9.z_ref, f32[1,512]{1,0:T(1,128)S(1)} %get-tuple-element.10.lse_ref, bf16[512,256]{1,0:T(8,128)(2,1)S(1)} %get-tuple-element.11.next_ref), custom_call_target="tpu_custom_call" | custom-call | tf_op jit(solution)/shard_map/pallas_call | solution.py:660

commit v11 on v10

--- a/solution.py
+++ b/solution.py
@@ -17,7 +17,7 @@
 OPP, LEFT, RIGHT, OWN = 0, 1, 2, 3
 SIDE = 4
 N_HOP = 5
-FIRST = 1
+FIRST = 2
 STEP_OF_SLOT = (2, 3, 1, 0)
 
 
@@ -78,8 +78,8 @@
         return (off if isinstance(i, int) else pl.multiple_of(off, 16)), CHUNK
 
     barrier = pltpu.get_barrier_semaphore()
-    for j in range(1, n_tp):
-        pl.semaphore_signal(barrier, inc=1, device_id={"tp": lax.rem(tp + j, n_tp)}, device_id_type=MESH)
+    for peer in (left, right, partner):
+        pl.semaphore_signal(barrier, inc=1, device_id=peer, device_id_type=MESH)
     tell_near(barrier)
 
     parts = ((tail0, small), (0, tail0), (0, n_block))
@@ -114,8 +114,8 @@
     hid_copy.wait()
     h_t = hid_ref[...].astype(F32).T
     hx[0, :, 0:rows] = h_t
-    st_ln[tp, :, 0:rows] = jnp.sum(h_t, axis=0, keepdims=True)
-    st_ln[tp, :, rows:2 * rows] = jnp.sum(h_t * h_t, axis=0, keepdims=True)
+    st_ln[core, :, 0:rows] = jnp.sum(h_t, axis=0, keepdims=True)
+    st_ln[core, :, rows:2 * rows] = jnp.sum(h_t * h_t, axis=0, keepdims=True)
 
     def convert(slot, q):
         off, n = parts[q]
@@ -143,7 +143,7 @@
             send_sem=raw_send, recv_sem=raw_recv.at[int(slot == LEFT)],
             device_id={"tp": to}, device_id_type=MESH)
 
-    pl.semaphore_wait(barrier, n_tp - 1 + n_near)
+    pl.semaphore_wait(barrier, 3 + n_near)
 
     def tp_start(buf, stage):
         for j in range(1, n_tp):
@@ -157,10 +157,16 @@
     def tp_drain(buf):
         total_send(buf.at[pl.ds(0, n_tp - 1)], t_send)
 
-    tp_start(st_ln, 0)
-    for other in (False, True):
-        for slot in (RIGHT, LEFT):
-            raw_copy(slot, other).start()
+    def stat_copy(slot, to, sem):
+        return pltpu.make_async_remote_copy(
+            src_ref=st_ln.at[slot], dst_ref=st_ln.at[slot], send_sem=t_send, recv_sem=t_recv.at[sem],
+            device_id=to, device_id_type=MESH)
+
+    stat_copy(core, partner, 3).start()
+    for slot in (RIGHT, LEFT):
+        raw_copy(slot, False).start()
+    for peer in (left, right, partner):
+        pl.semaphore_signal(hop.at[N_HOP], inc=1, device_id=peer, device_id_type=MESH)
 
     total_load(vec_ref, in_sem.at[2])
     hx[0, :, rows:rows + LANE] = jnp.broadcast_to(vec_ref[0], (LANE, width)).T
@@ -181,6 +187,16 @@
     for q in range(2):
         convert(OPP, q)
         ex_copy(OPP, q, q).start()
+
+    pl.semaphore_wait(hop.at[N_HOP], 3)
+    total_recv(st_ln.at[0], t_recv.at[3])
+    mine_at = n_chip + chip
+    st_ln[mine_at] = st_ln[0] + st_ln[1]
+    for peer in (left, right, {"tp": lax.rem(tp + n_chip, n_tp)}):
+        stat_copy(mine_at, peer, 0).start()
+    for slot in (RIGHT, LEFT):
+        raw_copy(slot, True).start()
+
     for slot in (LEFT, RIGHT):
         ex_copy(slot, 0, 2).start()
     sides = e_oth.at[pl.ds(LEFT, 2), pl.ds(0, tail0), :]
@@ -192,10 +208,10 @@
     convert(OWN, 2)
     ex_copy(OWN, 2, 4).start()
 
-    tp_wait(st_ln, 0)
-    total = st_ln[0]
-    for j in range(1, n_tp):
-        total = total + st_ln[j]
+    total_recv(st_ln.at[pl.ds(0, 3)], t_recv.at[0])
+    total = st_ln[n_chip]
+    for j in range(1, n_chip):
+        total = total + st_ln[n_chip + j]
     mean = total[:, 0:rows] / full_width
     rstd = lax.rsqrt(total[:, rows:2 * rows] / full_width - mean * mean + NORM_EPS)
 
@@ -393,7 +409,7 @@
         ag_buf[vp] = tot
         lane = lax.broadcasted_iota(jnp.int32, (slab, LANE), 1)
         both = jnp.where(lane == 0, jnp.sum(tot, axis=1, keepdims=True), jnp.sum(tot * tot, axis=1, keepdims=True)).T
-        tp_drain(st_ln)
+        total_send(st_ln.at[pl.ds(0, 4)], t_send)
         row_st[tp] = jnp.zeros((1, 256), F32)
         row_st[tp, :, 0:slab] = both[0:1]
         row_st[tp, :, LANE:LANE + slab] = both[1:2]
@@ -495,13 +511,13 @@
     put(st_lse, tp, top + jnp.log(jnp.sum(s_acc[...] * jnp.exp(m8 - top), axis=0, keepdims=True)))
 
     me = vp * n_tp + tp
-    is_first = me == FIRST
-
-    @pl.when(jnp.logical_not(is_first))
-    def _():
-        pltpu.make_async_remote_copy(
-            src_ref=st_lse.at[tp], dst_ref=st_dir.at[me], send_sem=raw_send, recv_sem=d_recv,
-            device_id={"vp": FIRST // n_tp, "tp": FIRST % n_tp}, device_id_type=MESH).start()
+    is_first = me < FIRST
+    for first in range(FIRST):
+        @pl.when(me != first)
+        def _(first=first):
+            pltpu.make_async_remote_copy(
+                src_ref=st_lse.at[tp], dst_ref=st_dir.at[me], send_sem=raw_send, recv_sem=d_recv,
+                device_id={"vp": 0, "tp": first}, device_id_type=MESH).start()
 
     def collect(to_chip):
         return pltpu.make_async_remote_copy(
@@ -526,19 +542,18 @@
             src_ref=st_all.at[vp], dst_ref=st_all.at[vp], send_sem=v_send, recv_sem=v_recv.at[2],
             device_id={"vp": to, "tp": chip * 2 + to_core}, device_id_type=MESH)
 
-    def is_first_at(to, to_core):
-        return jnp.logical_and(to == FIRST // n_tp, chip * 2 + to_core == FIRST % n_tp)
-
     @pl.when(core == 1)
     def _():
         total_recv(st_lse.at[pl.ds(0, n_tp - 1)], t_recv.at[2])
         st_all[vp] = merge(st_lse, n_tp)
         for to in range(n_vp):
-            @pl.when(jnp.logical_and(vp != to, jnp.logical_not(is_first_at(to, 1))))
+            @pl.when(jnp.logical_and(vp != to, jnp.logical_or(chip != 0, to != 0)))
             def _(to=to):
                 spread(to, 1).start()
         for to in range(n_vp):
-            spread(to, 0).start()
+            @pl.when(jnp.logical_or(chip != 0, to != 0))
+            def _(to=to):
+                spread(to, 0).start()
         total_send(st_lse.at[pl.ds(0, n_chip - 1)], t_send)
 
         @pl.when(jnp.logical_not(is_first))
@@ -548,7 +563,10 @@
     @pl.when(core == 0)
     def _():
         total_send(st_lse.at[pl.ds(0, n_chip)], t_send)
-        total_recv(st_all.at[pl.ds(0, n_vp)], v_recv.at[2])
+
+        @pl.when(jnp.logical_not(is_first))
+        def _():
+            total_recv(st_all.at[pl.ds(0, n_vp)], v_recv.at[2])
 
     def result(value):
         for k in range(rows // LANE):
@@ -560,22 +578,18 @@
         st_dir[me] = put_row
         total_recv(st_dir.at[pl.ds(0, n_vp * n_tp - 1)], d_recv)
         result(merge(st_dir, n_vp * n_tp))
+        total_send(st_lse.at[pl.ds(0, FIRST - 1)], raw_send)
 
     @pl.when(jnp.logical_not(is_first))
     def _():
         result(merge(st_all, n_vp))
-        total_send(st_lse.at[pl.ds(0, 1)], raw_send)
+        total_send(st_lse.at[pl.ds(0, FIRST)], raw_send)
 
     sends = 2 * n_vp - 1
-    short = jnp.logical_and(chip == FIRST % n_tp // 2, vp != FIRST // n_tp)
-
-    @pl.when(jnp.logical_and(core == 1, short))
-    def _():
-        total_send(st_all.at[pl.ds(0, sends - 1)], v_send)
-
-    @pl.when(jnp.logical_and(core == 1, jnp.logical_not(short)))
-    def _():
-        total_send(st_all.at[pl.ds(0, sends)], v_send)
+    for there, fewer in ((chip != 0, 0), (jnp.logical_and(chip == 0, vp == 0), 1), (jnp.logical_and(chip == 0, vp != 0), 2)):
+        @pl.when(jnp.logical_and(core == 1, there))
+        def _(fewer=fewer):
+            total_send(st_all.at[pl.ds(0, sends - fewer)], v_send)
 
 
 def finish_kernel(n_piece, z_ref, lse_ref, next_ref, out_ref, sum_ref, row_ref, buf, sems):
@@ -644,8 +658,8 @@
                 pltpu.VMEM((2, 2, width, rows), BF16),
                 dma((7,)), dma, dma((5,)), dma, dma,
                 dma, dma((n_round,)), dma, dma, dma((n_round,)),
-                dma, dma((3,)), dma, dma((4,)), dma, dma((2,)), dma((2,)), dma, dma,
-                pltpu.SemaphoreType.REGULAR((N_HOP,)),
+                dma, dma((4,)), dma, dma((4,)), dma, dma((2,)), dma((2,)), dma, dma,
+                pltpu.SemaphoreType.REGULAR((N_HOP + 1,)),
                 pltpu.VMEM((rows, width), BF16),
                 pltpu.VMEM((1, rows), jnp.int32),
                 pltpu.VMEM((4, 1, width), F32),

time: 150 us -> 148 us (0.987)
  no operation moved by 1% of the time
where the time goes in v11:
time: 148 us
  Pallas kernels  147 us (99%)
    pallas_call x1, Pallas kernels, per_device(): pl.pallas_call(functools.partial(head_kernel, n_vp, n_tp, n_block, width...  145 us

profile of v11, /device:TPU:1, one launch (start us, length us, event | category | flops | bytes accessed | tf_op | source)
XLA Modules:
  0.0 148.1 jit_solution(846621320215270559)
XLA Ops:
  0.6 145.3 %shard_map.94 = (f32[1960,512]{1,0:T(8,128)S(1)}, f32[1,512]{1,0:T(1,128)S(1)}, bf16[512,256]{1,0:T(8,128)(2,1)S(1)}) custom-call(bf16[512,256]{1,0:T(8,128)(2,1)} %hid_hbm.1, f32[1,256]{1,0:T(1,128)} %bitcast.10, f32[1,256]{1,0:T(1,128)} %bitcast.11, bf16[15680,256]{1,0:T(8,128)(2,1)} %emb_ref.1, s32[1,512]{1,0:T(1,128)} %bitcast.8, f32[1,256]{1,0:T(1,128)} %bitcast.12, ...), custom_call_target="tpu_custom_call" | custom-call | flops 8220835840 | bytes 64225280 | tf_op jit(solution)/shard_map/pallas_call | solution.py:627
  146.0 2.1 %shard_map.95 = (f32[1960,512]{1,0:T(8,128)}, f32[1,512]{1,0:T(1,128)}, bf16[512,256]{1,0:T(8,128)(2,1)}) custom-call(f32[1960,512]{1,0:T(8,128)S(1)} %get-tuple-element.9.z_ref, f32[1,512]{1,0:T(1,128)S(1)} %get-tuple-element.10.lse_ref, bf16[512,256]{1,0:T(8,128)(2,1)S(1)} %get-tuple-element.11.next_ref), custom_call_target="tpu_custom_call" | custom-call | tf_op jit(solution)/shard_map/pallas_call | solution.py:674

commit v12 on v11

--- a/solution.py
+++ b/solution.py
@@ -63,7 +63,8 @@
             tell_near(hop.at[step + 1])
 
     n_carry = n_vp // 2
-    carries = vp < n_carry
+    carries = jnp.logical_or(vp < n_carry - 1, vp == n_carry)
+    own_slab = pl.ds(pl.multiple_of(lax.min(vp, n_carry - 1) * xslab, 32), xslab)
     half = (n_block // 2) // CHUNK
     n_round = half + 1
     small = n_block - 2 * half * CHUNK
@@ -224,7 +225,7 @@
 
     def slab_copy(d):
         return pltpu.make_async_remote_copy(
-            src_ref=slab_src, dst_ref=nb.at[d, pl.ds(pl.multiple_of(vp * xslab, 8), xslab), :],
+            src_ref=slab_src, dst_ref=nb.at[d, own_slab, :],
             send_sem=hx_send, recv_sem=sx_recv.at[d], device_id=right if d == 0 else left, device_id_type=MESH)
 
     norm(0)
@@ -232,7 +233,7 @@
 
     @pl.when(carries)
     def _():
-        slab_src[...] = xn[0, pl.ds(pl.multiple_of(vp * xslab, 32), xslab), :].astype(F32)
+        slab_src[...] = xn[0, own_slab, :].astype(F32)
         for d in range(2):
             slab_copy(d).start()
 
@@ -363,11 +364,10 @@
 
         @pl.when(carries)
         def _():
-            own = pl.ds(pl.multiple_of(vp * xslab, 8), xslab)
             for d in range(2):
                 slab_copy(d).wait_recv()
                 for j in range(1, n_vp):
-                    v_copy(nb.at[d, own, :], nb.at[d, own, :], 3, j).start()
+                    v_copy(nb.at[d, own_slab, :], nb.at[d, own_slab, :], 3, j).start()
 
     nb_copy = pltpu.make_async_remote_copy(
         src_ref=nb, dst_ref=nb_par, send_sem=hx_send, recv_sem=nb_recv, device_id=partner, device_id_type=MESH)
@@ -512,7 +512,7 @@
 
     me = vp * n_tp + tp
     is_first = me < FIRST
-    for first in range(FIRST):
+    for first in reversed(range(FIRST)):
         @pl.when(me != first)
         def _(first=first):
             pltpu.make_async_remote_copy(

time: 148 us -> 148 us (level)
  no operation moved by 1% of the time
where the time goes in v12:
time: 148 us
  Pallas kernels  147 us (99%)
    pallas_call x1, Pallas kernels, per_device(): pl.pallas_call(functools.partial(head_kernel, n_vp, n_tp, n_block, width...  145 us

profile of v12, /device:TPU:1, one launch (start us, length us, event | category | flops | bytes accessed | tf_op | source)
XLA Modules:
  0.0 148.0 jit_solution(9165750139033990023)
XLA Ops:
  0.6 145.3 %shard_map.94 = (f32[1960,512]{1,0:T(8,128)S(1)}, f32[1,512]{1,0:T(1,128)S(1)}, bf16[512,256]{1,0:T(8,128)(2,1)S(1)}) custom-call(bf16[512,256]{1,0:T(8,128)(2,1)} %hid_hbm.1, f32[1,256]{1,0:T(1,128)} %bitcast.10, f32[1,256]{1,0:T(1,128)} %bitcast.11, bf16[15680,256]{1,0:T(8,128)(2,1)} %emb_ref.1, s32[1,512]{1,0:T(1,128)} %bitcast.8, f32[1,256]{1,0:T(1,128)} %bitcast.12, ...), custom_call_target="tpu_custom_call" | custom-call | flops 8220835840 | bytes 64225280 | tf_op jit(solution)/shard_map/pallas_call | solution.py:627
  145.9 2.1 %shard_map.95 = (f32[1960,512]{1,0:T(8,128)}, f32[1,512]{1,0:T(1,128)}, bf16[512,256]{1,0:T(8,128)(2,1)}) custom-call(f32[1960,512]{1,0:T(8,128)S(1)} %get-tuple-element.9.z_ref, f32[1,512]{1,0:T(1,128)S(1)} %get-tuple-element.10.lse_ref, bf16[512,256]{1,0:T(8,128)(2,1)S(1)} %get-tuple-element.11.next_ref), custom_call_target="tpu_custom_call" | custom-call | tf_op jit(solution)/shard_map/pallas_call | solution.py:674

commit v13 on v12

--- a/solution.py
+++ b/solution.py
@@ -94,12 +94,12 @@
 
     hid_copy = pltpu.make_async_copy(hid_hbm, hid_ref, in_sem.at[0])
     tok_copy = pltpu.make_async_copy(tok_hbm, tok_ref, in_sem.at[1])
+    for slot in (RIGHT, LEFT):
+        load(slot, True, 0, 0).start()
+        load(slot, False, 0, 0).start()
     hid_copy.start()
     for k, src in enumerate((g_hbm, b_hbm, eg_hbm, eb_hbm)):
         pltpu.make_async_copy(src, vec_ref.at[k], in_sem.at[2]).start()
-    for slot in (RIGHT, LEFT):
-        load(slot, True, 0, 0).start()
-        load(slot, False, 0, 0).start()
 
     def total_load(ref, sem):
         pltpu.make_async_copy(ref, ref, sem).wait()
@@ -111,12 +111,6 @@
     def total_send(ref, sem):
         pltpu.make_async_remote_copy(src_ref=ref, dst_ref=ref, send_sem=sem, recv_sem=sem,
                                      device_id=partner, device_id_type=MESH).wait_send()
-
-    hid_copy.wait()
-    h_t = hid_ref[...].astype(F32).T
-    hx[0, :, 0:rows] = h_t
-    st_ln[core, :, 0:rows] = jnp.sum(h_t, axis=0, keepdims=True)
-    st_ln[core, :, rows:2 * rows] = jnp.sum(h_t * h_t, axis=0, keepdims=True)
 
     def convert(slot, q):
         off, n = parts[q]
@@ -163,12 +157,18 @@
             src_ref=st_ln.at[slot], dst_ref=st_ln.at[slot], send_sem=t_send, recv_sem=t_recv.at[sem],
             device_id=to, device_id_type=MESH)
 
-    stat_copy(core, partner, 3).start()
     for slot in (RIGHT, LEFT):
         raw_copy(slot, False).start()
     for peer in (left, right, partner):
         pl.semaphore_signal(hop.at[N_HOP], inc=1, device_id=peer, device_id_type=MESH)
 
+    hid_copy.wait()
+    h_t = hid_ref[...].astype(F32).T
+    hx[0, :, 0:rows] = h_t
+    st_ln[core, :, 0:rows] = jnp.sum(h_t, axis=0, keepdims=True)
+    st_ln[core, :, rows:2 * rows] = jnp.sum(h_t * h_t, axis=0, keepdims=True)
+
+    stat_copy(core, partner, 3).start()
     total_load(vec_ref, in_sem.at[2])
     hx[0, :, rows:rows + LANE] = jnp.broadcast_to(vec_ref[0], (LANE, width)).T
     hx[0, :, rows + LANE:rows + 256] = jnp.broadcast_to(vec_ref[1], (LANE, width)).T
@@ -594,10 +594,11 @@
 
 def finish_kernel(n_piece, z_ref, lse_ref, next_ref, out_ref, sum_ref, row_ref, buf, sems):
     lse = lse_ref[...]
-    n = z_ref.shape[0] // n_piece
+    unit = z_ref.shape[0] // 35
+    edges = [unit * k for k in (0, 1, 3, 7, 14, 21, 28, 35)]
 
     def put(j):
-        part = pl.ds(j * n, n)
+        part = pl.ds(edges[j], edges[j + 1] - edges[j])
         return pltpu.make_async_copy(buf.at[part, :], out_ref.at[part, :], sems.at[j])
 
     small = [pltpu.make_async_copy(lse_ref, sum_ref, sems.at[n_piece]),
@@ -605,7 +606,7 @@
     for copy in small:
         copy.start()
     for j in range(n_piece):
-        buf[j * n:(j + 1) * n, :] = z_ref[j * n:(j + 1) * n, :] - lse
+        buf[edges[j]:edges[j + 1], :] = z_ref[edges[j]:edges[j + 1], :] - lse
         put(j).start()
     for copy in small:
         copy.wait()
@@ -670,7 +671,7 @@
             cost_estimate=pl.CostEstimate(
                 flops=4 * rows * n_block * n_tp * width, bytes_accessed=16 * n_block * n_tp * width, transcendentals=rows * n_block),
         )(hidden, lnf_gain[None, :], lnf_bias[None, :], emb_table, next_tok[None, :], eln_gain[None, :], eln_bias[None, :])
-        n_piece = 5
+        n_piece = 7
         logprobs_t, log_sum, next_bf = pl.pallas_call(
             functools.partial(finish_kernel, n_piece),
             out_shape=(

time: 148 us -> 148 us (level)
  no operation moved by 1% of the time
where the time goes in v13:
time: 148 us
  Pallas kernels  147 us (99%)
    pallas_call x1, Pallas kernels, per_device(): pl.pallas_call(functools.partial(head_kernel, n_vp, n_tp, n_block, width...  145 us

profile of v13, /device:TPU:1, one launch (start us, length us, event | category | flops | bytes accessed | tf_op | source)
XLA Modules:
  0.0 148.0 jit_solution(1697727591874820752)
XLA Ops:
  0.6 145.3 %shard_map.94 = (f32[1960,512]{1,0:T(8,128)S(1)}, f32[1,512]{1,0:T(1,128)S(1)}, bf16[512,256]{1,0:T(8,128)(2,1)S(1)}) custom-call(bf16[512,256]{1,0:T(8,128)(2,1)} %hid_hbm.1, f32[1,256]{1,0:T(1,128)} %bitcast.10, f32[1,256]{1,0:T(1,128)} %bitcast.11, bf16[15680,256]{1,0:T(8,128)(2,1)} %emb_ref.1, s32[1,512]{1,0:T(1,128)} %bitcast.8, f32[1,256]{1,0:T(1,128)} %bitcast.12, ...), custom_call_target="tpu_custom_call" | custom-call | flops 8220835840 | bytes 64225280 | tf_op jit(solution)/shard_map/pallas_call | solution.py:628
  145.9 2.1 %shard_map.95 = (f32[1960,512]{1,0:T(8,128)}, f32[1,512]{1,0:T(1,128)}, bf16[512,256]{1,0:T(8,128)(2,1)}) custom-call(f32[1960,512]{1,0:T(8,128)S(1)} %get-tuple-element.9.z_ref, f32[1,512]{1,0:T(1,128)S(1)} %get-tuple-element.10.lse_ref, bf16[512,256]{1,0:T(8,128)(2,1)S(1)} %get-tuple-element.11.next_ref), custom_call_target="tpu_custom_call" | custom-call | tf_op jit(solution)/shard_map/pallas_call | solution.py:675

commit v14 on v13

--- a/solution.py
+++ b/solution.py
@@ -68,13 +68,13 @@
     half = (n_block // 2) // CHUNK
     n_round = half + 1
     small = n_block - 2 * half * CHUNK
-    small1 = (small // 16) * 8
-    small2 = small - small1
+    small2 = (small // 16) * 8
+    small1 = small - small2
     tail0 = 2 * half * CHUNK
 
     def piece(h, i):
         if isinstance(i, int) and i == 0:
-            return (tail0, small1) if h == 0 else (tail0 + small1, small2)
+            return (tail0 + small2, small1) if h == 0 else (tail0, small2)
         off = h * half * CHUNK + (i - 1) * CHUNK
         return (off if isinstance(i, int) else pl.multiple_of(off, 16)), CHUNK
 
@@ -651,8 +651,8 @@
                 pltpu.VMEM((n_vp, slab, width), F32),
                 pltpu.VMEM((n_vp * n_tp, rows // LANE, LANE), F32),
                 pltpu.VMEM((small, width), F32),
+                pltpu.VMEM((2, small - small // 16 * 8, width), F32),
                 pltpu.VMEM((2, small // 16 * 8, width), F32),
-                pltpu.VMEM((2, small - small // 16 * 8, width), F32),
                 pltpu.VMEM((width // (n_vp // 2), rows), F32),
                 pltpu.VMEM((2, width, rows), F32),
                 pltpu.VMEM((2, width, rows), F32),

time: 148 us -> 148 us (level)
  no operation moved by 1% of the time
where the time goes in v14:
time: 148 us
  Pallas kernels  148 us (100%)
    pallas_call x1, Pallas kernels, per_device(): pl.pallas_call(functools.partial(head_kernel, n_vp, n_tp, n_block, width...  146 us

profile of v14, /device:TPU:1, one launch (start us, length us, event | category | flops | bytes accessed | tf_op | source)
XLA Modules:
  0.0 148.3 jit_solution(9212565063118382154)
XLA Ops:
  0.6 145.6 %shard_map.94 = (f32[1960,512]{1,0:T(8,128)S(1)}, f32[1,512]{1,0:T(1,128)S(1)}, bf16[512,256]{1,0:T(8,128)(2,1)S(1)}) custom-call(bf16[512,256]{1,0:T(8,128)(2,1)} %hid_hbm.1, f32[1,256]{1,0:T(1,128)} %bitcast.10, f32[1,256]{1,0:T(1,128)} %bitcast.11, bf16[15680,256]{1,0:T(8,128)(2,1)} %emb_ref.1, s32[1,512]{1,0:T(1,128)} %bitcast.8, f32[1,256]{1,0:T(1,128)} %bitcast.12, ...), custom_call_target="tpu_custom_call" | custom-call | flops 8220835840 | bytes 64225280 | tf_op jit(solution)/shard_map/pallas_call | solution.py:628
  146.2 2.1 %shard_map.95 = (f32[1960,512]{1,0:T(8,128)}, f32[1,512]{1,0:T(1,128)}, bf16[512,256]{1,0:T(8,128)(2,1)}) custom-call(f32[1960,512]{1,0:T(8,128)S(1)} %get-tuple-element.9.z_ref, f32[1,512]{1,0:T(1,128)S(1)} %get-tuple-element.10.lse_ref, bf16[512,256]{1,0:T(8,128)(2,1)S(1)} %get-tuple-element.11.next_ref), custom_call_target="tpu_custom_call" | custom-call | tf_op jit(solution)/shard_map/pallas_call | solution.py:675
